TPU v7x, 32 devices: a whole 2x2x4 slice. The times are simulated.
32 devices in a mesh: up: 8 (over z, core), down: 4 (over y, x).
Axes of the slice: x: 2, y: 2, z: 4, core: 2. Of those that a mesh axis runs over, the one named last changes fastest.
Arguments:
- deltas: bfloat16 [256, 4096], P('down', 'up'), may hold values from -6 to 6
- gradients: bfloat16 [256, 4096], P('up', 'down'), may hold values from -0.375 to 0.375
- up_blocks: int32 [8, 16], P(None, 'up'), may hold values from 0 to 3, as said below
- down_blocks: int32 [16], P('down'), may hold values from 0 to 7, as said below
- decoder: bfloat16 [4096, 4608], P('up', 'down'), may hold values from -0.09375 to 0.09375
- encoder: bfloat16 [4608, 4096], P('up', 'down'), may hold values from -6 to 6
Outputs:
- edge_scores: float32 [4096, 4096], P('up', 'down')
Inputs may be any that keep to these rules, and one draw needn't show every extreme that they name: `up_blocks`: for each window and each index i of up, the 2 entries in columns i * 2 to (i + 1) * 2 - 1 are distinct. `down_blocks`: for each index j of down, the 4 entries j * 4 to (j + 1) * 4 - 1 are distinct.
All inputs are finite; a program needn't handle non-finite values.
Results may differ from a plain program's by a relative error of at most 0.0003.
Values may be sent and summed in bfloat16 or wider, within the bound.
A program may use at most 64 MiB of HBM per device.

v0:
```python
import functools

import jax
import jax.numpy as jnp
from jax import lax
from jax.experimental import pallas as pl
from jax.experimental.pallas import tpu as pltpu
from jax.sharding import PartitionSpec as P

BLOCK = 128
LARGE, SMALL = 24 << 20, 4 << 20
MESH = pl.DeviceIdType.MESH
F32 = jnp.float32


def flag(number, block, kind):
    return jnp.where(jnp.full((1, BLOCK), number, jnp.int32) == block, 1.0, 0.0).astype(kind)


def pick(ref, rows, number, blocks):
    total = None
    for b in range(blocks):
        term = ref[rows, b * BLOCK:(b + 1) * BLOCK] * flag(number, b, ref.dtype)
        total = term if total is None else total + term
    return total


def gather_scores(
    n_up, n_down, upb, downb, deltas, grads, dec, enc, out,
    dec_all, enc_raw, enc_all, del_raw, del_all, grad_raw, grad_all, masked, acc, prod, res,
    load_sem, dec_send, dec_recv, del_send, del_recv, enc_send, enc_recv,
    grad_send, grad_recv, pair_send, pair_recv, pg_send, pg_recv, out_sem,
):
    levels = n_up // 2
    rows, depth = dec.shape
    height = enc.shape[0]
    half = enc_all.shape[2]
    chunk = rows // 4
    toks = grads.shape[0]
    wins = del_all.shape[1]
    win = del_all.shape[2]
    uact = upb.shape[0]
    dact = downb.shape[0]
    up, down = lax.axis_index("up"), lax.axis_index("down")
    z, core = up // 2, up % 2
    place = lambda d: 2 * (d // 2) + (d + d // 2) % 2
    pos = place(down)
    right, left = place((pos + 1) % 4), place((pos + 3) % 4)
    diag = place((pos + 2) % 4)
    ring_to = ((up, right), (up, left))
    ring_from = (left, right)
    step_of = (1, -1)

    loads = [
        pltpu.make_async_copy(dec, dec_all.at[down], load_sem.at[0]),
        pltpu.make_async_copy(enc, enc_raw, load_sem.at[1]),
        pltpu.make_async_copy(deltas, del_raw, load_sem.at[2]),
        pltpu.make_async_copy(grads, grad_raw, load_sem.at[3]),
    ]
    for copy in loads:
        copy.start()

    barrier = pltpu.get_barrier_semaphore()
    can_go = (z < levels - 1, z > 0)
    for dev in (*ring_to, (2 * z + 1 - core, down)):
        pl.semaphore_signal(barrier, inc=1, device_id=dev, device_id_type=MESH)
    for r in range(2):
        @pl.when(can_go[r])
        def _():
            pl.semaphore_signal(barrier, inc=1, device_id=(up + 2 * step_of[r], down), device_id_type=MESH)

    loads[2].wait()
    for w in range(wins):
        for s in range(uact):
            del_all[down, w, :, s * BLOCK:(s + 1) * BLOCK] = pick(
                del_raw, slice(w * win, (w + 1) * win), upb[s, down * wins + w], rows // BLOCK)
    loads[3].wait()
    loads[1].wait()
    for s in range(dact):
        grad_all[pl.ds(pl.multiple_of(up * toks, toks), toks), s * BLOCK:(s + 1) * BLOCK] = pick(
            grad_raw, slice(0, toks), downb[s], enc.shape[1] // BLOCK)
        side, at = divmod(s * BLOCK, half)
        enc_all[side, pl.ds(pl.multiple_of(up * height, 16), height), at:at + BLOCK] = pick(
            enc_raw, slice(0, height), downb[s], enc.shape[1] // BLOCK)
    loads[0].wait()
    expected = 3 + jnp.where(z < levels - 1, 1, 0) + jnp.where(z > 0, 1, 0)
    pl.semaphore_wait(barrier, expected)

    orders = ((0, 2, 1, 3), (1, 3, 0, 2))

    def dec_copy(r, i, owner):
        piece = orders[r][i % 4]
        ref = dec_all.at[owner, pl.ds(piece * chunk, chunk)]
        return pltpu.make_async_remote_copy(
            ref, ref, dec_send.at[r, i], dec_recv.at[r, i], device_id=ring_to[r], device_id_type=MESH)

    def del_copy(r, i, owner):
        piece = (i + r) % 2
        ref = del_all.at[owner, piece]
        return pltpu.make_async_remote_copy(
            ref, ref, del_send.at[r, i], del_recv.at[r, i], device_id=ring_to[r], device_id_type=MESH)

    def enc_rows(level, h, c):
        return enc_all.at[h, pl.ds(pl.multiple_of((level * 2 + c) * height, 16), height)]

    def enc_copy(r, k, level):
        ref = enc_rows(level, (k - 1) % 2, core)
        return pltpu.make_async_remote_copy(
            ref, ref, enc_send.at[r, k - 1], enc_recv.at[r, k - 1],
            device_id=(up + 2 * step_of[r], down), device_id_type=MESH)

    def grad_rows(level, c):
        return grad_all.at[pl.ds(pl.multiple_of((level * 2 + c) * toks, toks), toks)]

    def grad_copy(r, j, level):
        ref = grad_rows(level, core)
        return pltpu.make_async_remote_copy(
            ref, ref, grad_send.at[r, j - 1], grad_recv.at[r, j - 1],
            device_id=(up + 2 * step_of[r], down), device_id_type=MESH)

    def pair_copy(level, h, c):
        ref = enc_rows(level, h, c)
        return pltpu.make_async_remote_copy(
            ref, ref, pair_send.at[level, h], pair_recv.at[level, h],
            device_id=(2 * z + 1 - core, down), device_id_type=MESH)

    def pair_grad(level, c):
        ref = grad_rows(level, c)
        return pltpu.make_async_remote_copy(
            ref, ref, pg_send.at[level], pg_recv.at[level],
            device_id=(2 * z + 1 - core, down), device_id_type=MESH)

    inside = lambda level: jnp.logical_and(level >= 0, level < levels)

    for r in range(2):
        del_copy(r, 0, down).start()
        del_copy(r, 1, down).start()

        @pl.when(can_go[r])
        def _():
            grad_copy(r, 1, z).start()
    for i in range(2):
        for r in range(2):
            dec_copy(r, i, down).start()

            @pl.when(can_go[r])
            def _():
                enc_copy(r, i + 1, z).start()
    for i in range(2, 4):
        for r in range(2):
            dec_copy(r, i, down).start()
    pair_grad(z, core).start()
    for h in range(2):
        pair_copy(z, h, core).start()

    part = rows // 2

    def product_unit(u, low, high):
        q, m, n = u // 4, u // 2 % 2, u % 2
        gap = jnp.maximum(q - z, z - q)
        enc_hop = jnp.where(gap == 0, 0, 2 * gap - 1 + n)
        dec_hop = jnp.where(q == diag, 5 + m, 4)
        hop = jnp.maximum(enc_hop, dec_hop)

        @pl.when(jnp.logical_and(hop >= low, hop <= high))
        def _():
            rs = pl.ds(pl.multiple_of(m * part, part), part)
            acc[n, rs] += jnp.dot(
                dec_all[q, rs, :], enc_all[n, pl.ds(pl.multiple_of(q * depth, 128), depth), :],
                preferred_element_type=F32)

    def products(low, high):
        pl.loop(0, 4 * levels)(lambda u: product_unit(u, low, high))

    def pair_wait(low, high):
        for lv in range(levels):
            for h in range(2):
                gap = jnp.maximum(lv - z, z - lv)
                hop = jnp.where(gap == 0, 0, 2 * gap - 1 + h)

                @pl.when(jnp.logical_and(hop >= low, hop <= high))
                def _():
                    pair_copy(lv, h, 1 - core).wait_recv()

    acc[...] = jnp.zeros_like(acc)

    for k in range(1, 2 * (levels - 1) + 1):
        j, h = (k + 1) // 2, (k - 1) % 2
        for r in range(2):
            if k == 1:
                del_copy(r, 0, ring_from[r]).wait_recv()
                del_copy(r, 2, ring_from[r]).start()
            if k <= 2:
                dec_copy(r, k - 1, ring_from[r]).wait_recv()
                dec_copy(r, k + 3, ring_from[r]).start()
        for r in range(2):
            level = z - step_of[r] * j

            @pl.when(inside(level))
            def _():
                if h == 0:
                    grad_copy(r, j, level).wait_recv()
                    if j < levels - 1:
                        @pl.when(can_go[r])
                        def _():
                            grad_copy(r, j + 1, level).start()
                    pair_grad(level, core).start()
                enc_copy(r, k, level).wait_recv()
                if j < levels - 1:
                    @pl.when(can_go[r])
                    def _():
                        enc_copy(r, k + 2, level).start()
                pair_copy(level, h, core).start()
        if k == 2 * (levels - 2):
            for r in range(2):
                for i in range(2, 4):
                    dec_copy(r, i, ring_from[r]).wait_recv()
            pair_wait(0, 4)
            products(0, 4)
        if k == 2 * (levels - 2) + 1:
            for r in range(2):
                del_copy(r, 1, ring_from[r]).wait_recv()
                del_copy(r, 2, diag).wait_recv()
            for lv in range(levels):
                pair_grad(lv, 1 - core).wait_recv()
            for d in range(n_down):
                for w in range(wins):
                    for b in range(rows // BLOCK):
                        value = jnp.zeros((win, BLOCK), masked.dtype)
                        for s in range(uact):
                            on = flag(upb[s, d * wins + w], b, masked.dtype)
                            value = value + del_all[d, w, :, s * BLOCK:(s + 1) * BLOCK] * on
                        t = (d * wins + w) * win
                        masked[t:t + win, b * BLOCK:(b + 1) * BLOCK] = value
            prod[...] = lax.dot_general(
                masked[...], grad_all[...], (((0,), (0,)), ((), ())), preferred_element_type=F32)

            for r in range(2):
                dec_copy(r, 4, diag).wait_recv()
            pair_wait(5, 5)
            products(5, 5)

    for r in range(2):
        dec_copy(r, 5, diag).wait_recv()
    pair_wait(6, 6)
    products(6, 6)
    stores = []
    for s in range(dact):
        side, at = divmod(s * BLOCK, half)
        res[s] = acc[side, :, at:at + BLOCK] * prod[:, s * BLOCK:(s + 1) * BLOCK]
        stores.append(pltpu.make_async_copy(res.at[s], out.at[s], out_sem.at[s]))
        stores[-1].start()

    for r in range(2):
        for i in range(3):
            del_copy(r, i, down).wait_send()
        for i in range(6):
            dec_copy(r, i, down).wait_send()
        for k in range(1, 2 * (levels - 1) + 1):
            @pl.when(jnp.logical_and(can_go[r], inside(z - step_of[r] * ((k - 1) // 2))))
            def _():
                enc_copy(r, k, z).wait_send()
                if k % 2:
                    grad_copy(r, (k + 1) // 2, z).wait_send()
    for lv in range(levels):
        pair_grad(lv, core).wait_send()
        for h in range(2):
            pair_copy(lv, h, core).wait_send()
    for copy in stores:
        copy.wait()


def spread(downb, scored, out, blank, held, load_sem, out_sem, blank_sem):
    loads = [pltpu.make_async_copy(scored.at[s], held.at[s], load_sem.at[s]) for s in range(downb.shape[0])]
    for copy in loads:
        copy.start()
    blank[...] = jnp.zeros_like(blank)
    blocks = out.shape[1] // BLOCK

    def each_blank(act):
        for c in range(blocks):
            used = sum((downb[s] == c).astype(jnp.int32) for s in range(downb.shape[0]))

            @pl.when(used == 0)
            def _():
                act(pltpu.make_async_copy(blank, out.at[:, c * BLOCK:(c + 1) * BLOCK], blank_sem.at[c]))

    each_blank(lambda copy: copy.start())
    stores = []
    for s, copy in enumerate(loads):
        copy.wait()
        cols = pl.ds(pl.multiple_of(downb[s] * BLOCK, BLOCK), BLOCK)
        stores.append(pltpu.make_async_copy(held.at[s], out.at[:, cols], out_sem.at[s]))
        stores[-1].start()
    each_blank(lambda copy: copy.wait())
    for copy in stores:
        copy.wait()


def ring_local(n_up, n_down, win, deltas, gradients, up_blocks, down_blocks, decoder, encoder):
    rows, depth = decoder.shape
    height, cols = encoder.shape
    toks = gradients.shape[0]
    uact, dact = up_blocks.shape[1], down_blocks.shape[0]
    tokens = deltas.shape[0] * n_down
    wins = deltas.shape[0] // win
    used = dact * BLOCK
    levels = n_up // 2
    kind = decoder.dtype
    dma = pltpu.SemaphoreType.DMA
    smem, anywhere = pl.BlockSpec(memory_space=pltpu.SMEM), pl.BlockSpec(memory_space=pl.ANY)
    hbm = pl.BlockSpec(memory_space=pltpu.HBM)
    hops = 2 * (levels - 1)
    scored = pl.pallas_call(
        functools.partial(gather_scores, n_up, n_down),
        out_shape=jax.ShapeDtypeStruct((dact, rows, BLOCK), F32),
        in_specs=[smem, smem, hbm, hbm, hbm, hbm],
        out_specs=anywhere,
        scratch_shapes=[
            pltpu.VMEM((n_down, rows, depth), kind),
            pltpu.VMEM((height, cols), kind),
            pltpu.VMEM((2, n_up * height, used // 2), kind),
            pltpu.VMEM(deltas.shape, kind),
            pltpu.VMEM((n_down, wins, win, uact * BLOCK), kind),
            pltpu.VMEM((toks, cols), kind),
            pltpu.VMEM((n_up * toks, used), kind),
            pltpu.VMEM((tokens, rows), kind),
            pltpu.VMEM((2, rows, used // 2), F32),
            pltpu.VMEM((rows, used), F32),
            pltpu.VMEM((dact, rows, BLOCK), F32),
            dma((4,)),
            dma((2, 6)), dma((2, 6)),
            dma((2, 3)), dma((2, 3)),
            dma((2, hops)), dma((2, hops)),
            dma((2, levels - 1)), dma((2, levels - 1)),
            dma((levels, 2)), dma((levels, 2)),
            dma((levels,)), dma((levels,)),
            dma((dact,)),
        ],
        compiler_params=pltpu.CompilerParams(collective_id=0, has_side_effects=True, vmem_limit_bytes=LARGE),
        name="gather_scores",
    )(*[pltpu.with_memory_space_constraint(x, pltpu.HBM) for x in (up_blocks.T, down_blocks, deltas, gradients, decoder, encoder)])
    return pl.pallas_call(
        spread,
        out_shape=jax.ShapeDtypeStruct((rows, cols), F32),
        in_specs=[smem, anywhere],
        out_specs=anywhere,
        scratch_shapes=[
            pltpu.VMEM((rows, BLOCK), F32),
            pltpu.VMEM((dact, rows, BLOCK), F32),
            dma((dact,)), dma((dact,)), dma((cols // BLOCK,)),
        ],
        compiler_params=pltpu.CompilerParams(vmem_limit_bytes=SMALL),
        name="spread",
    )(pltpu.with_memory_space_constraint(down_blocks, pltpu.HBM), scored)


def plain_local(deltas, gradients, up_blocks, down_blocks, decoder, encoder):
    token_deltas = lax.all_gather(deltas, "down", axis=0, tiled=True)
    token_grads = lax.all_gather(gradients, "up", axis=0, tiled=True)
    tokens, rows = token_deltas.shape
    windows, dact = up_blocks.shape[0], down_blocks.shape[0]
    row_blocks, col_blocks = rows // BLOCK, encoder.shape[1] // BLOCK
    local_ids = jnp.arange(row_blocks, dtype=jnp.int32)
    block_on = jnp.any(up_blocks[:, :, None] == local_ids[None, None, :], axis=1)
    masked = token_deltas.reshape(windows, tokens // windows, row_blocks, BLOCK) * block_on[
        :, None, :, None].astype(token_deltas.dtype)
    masked = masked.reshape(tokens, rows)
    dec_whole = lax.all_gather(decoder, "down", axis=1, tiled=True)
    height = encoder.shape[0]
    enc_used = jnp.take(encoder.reshape(height, col_blocks, BLOCK), down_blocks, axis=1).reshape(height, dact * BLOCK)
    virtual = jnp.dot(dec_whole, lax.all_gather(enc_used, "up", axis=0, tiled=True), preferred_element_type=F32)
    grad_used = jnp.take(token_grads.reshape(tokens, col_blocks, BLOCK), down_blocks, axis=1).reshape(tokens, dact * BLOCK)
    product = lax.dot_general(masked, grad_used, (((0,), (0,)), ((), ())), preferred_element_type=F32)
    scored = (product * virtual).reshape(rows, dact, BLOCK)
    filled = jnp.zeros((rows, col_blocks, BLOCK), F32).at[:, down_blocks, :].set(scored)
    return filled.reshape(rows, encoder.shape[1])


def solution(mesh):
    n_up, n_down = mesh.shape["up"], mesh.shape["down"]
    ringed = n_down == 4 and n_up == 2 * n_down

    def local(deltas, gradients, up_blocks, down_blocks, decoder, encoder):
        args = (deltas, gradients, up_blocks, down_blocks, decoder, encoder)
        tokens = deltas.shape[0] * n_down
        win = tokens // up_blocks.shape[0]
        if ringed and deltas.shape[0] == 2 * win:
            return ring_local(n_up, n_down, win, *args)
        return plain_local(*args)

    placed = (P("down", "up"), P("up", "down"), P(None, "up"), P("down"), P("up", "down"), P("up", "down"))
    return jax.shard_map(local, mesh=mesh, in_specs=placed, out_specs=P("up", "down"), check_vma=False)
```

profile of v0, /device:TPU:0, one launch (start us, length us, event | category | flops | bytes accessed | tf_op | source)
XLA Modules:
  0.0 51.6 jit_solution(8075209616088913476)
XLA Ops:
  0.0 49.4 %gather_scores.1.scored = f32[4,512,128]{2,1,0:T(8,128)S(1)} custom-call(s32[2,8]{1,0:T(2,128)} %bitcast.1, s32[4]{0:T(128)} %downb.3, bf16[64,512]{1,0:T(8,128)(2,1)} %deltas.1, bf16[32,1024]{1,0:T(8,128)(2,1)} %grads.1, bf16[512,1152]{1,0:T(8,128)(2,1)} %dec.1, bf16[576,1024]{1,0:T(8,128)(2,1)} %enc.1), custom_call_target="tpu_custom_call" | custom-call | tf_op jit(solution)/shard_map/gather_scores/pallas_call | solution.py:314
  49.4 2.2 %spread.1 = f32[512,1024]{1,0:T(8,128)} custom-call(s32[4]{0:T(128)} %downb.3, f32[4,512,128]{2,1,0:T(8,128)S(1)} %gather_scores.1.scored), custom_call_target="tpu_custom_call" | custom-call | tf_op jit(solution)/shard_map/spread/pallas_call | solution.py:343
where the time goes:
time: 52.6 us; the launch traced here: 51.6 us
  Pallas kernels  51.6 us (98%)
    pallas_call x1, Pallas kernels, ring_local(): pl.pallas_call(functools.partial(gather_scores, n_up, n_down), out_shape=...  49.4 us
    pallas_call x1, Pallas kernels, ring_local(): pl.pallas_call(spread, out_shape=jax.ShapeDtypeStruct((rows, cols), F32),...  2.2 us

commit v1 on v0

v1 whole, which is shorter than its diff:
```python
import functools

import jax
import jax.numpy as jnp
from jax import lax
from jax.experimental import pallas as pl
from jax.experimental.pallas import tpu as pltpu
from jax.sharding import PartitionSpec as P

BLOCK = 128
TAIL = 256
LARGE = 24 << 20
MESH = pl.DeviceIdType.MESH
F32 = jnp.float32


def flag(number, block, kind):
    return jnp.where(jnp.full((1, BLOCK), number, jnp.int32) == block, 1.0, 0.0).astype(kind)


def pick(ref, rows, number, blocks):
    total = None
    for b in range(blocks):
        term = ref[rows, b * BLOCK:(b + 1) * BLOCK] * flag(number, b, ref.dtype)
        total = term if total is None else total + term
    return total


def gather_scores(
    n_up, n_down, upb_in, downb_in, deltas, grads, dec, enc, out,
    upb, downb, dec_all, enc_raw, enc_all, del_raw, del_all, grad_raw, grad_all, masked, acc, prod,
    load_sem, send_sem, dec_recv, del_recv, enc_recv, pair_recv, grad_recv,
):
    levels = n_up // 2
    rows, depth = dec.shape
    height = enc.shape[0]
    half = enc_all.shape[2]
    part = rows // 2
    piece = part // 2
    toks = grads.shape[0]
    wins = del_all.shape[1]
    win = del_all.shape[2]
    uact = upb.shape[0]
    dact = downb.shape[0]
    blocks = enc.shape[1] // BLOCK
    up, down = lax.axis_index("up"), lax.axis_index("down")
    z, core = up // 2, up % 2
    place = lambda d: 2 * (d // 2) + (d + d // 2) % 2
    pos = place(down)
    right, left = place((pos + 1) % 4), place((pos + 3) % 4)
    diag = place((pos + 2) % 4)
    ring_to = ((up, right), (up, left))
    ring_from = (left, right)
    step_of = (1, -1)
    pair = (2 * z + 1 - core, down)
    others = [(up, right), (up, left), (up, diag)]
    can_go = (z < levels - 1, z > 0)
    last = levels - 1
    at_end = jnp.logical_or(z == 0, z == last)
    inside = lambda level: jnp.logical_and(level >= 0, level < levels)
    levels_of = [(2 * ((z + i) % levels) + core, down) for i in range(1, levels)]

    barrier = pltpu.get_barrier_semaphore()
    for dev in (*others, pair, *levels_of):
        pl.semaphore_signal(barrier, inc=1, device_id=dev, device_id_type=MESH)

    loads = [
        pltpu.make_async_copy(downb_in, downb, load_sem.at[0]),
        pltpu.make_async_copy(enc, enc_raw, load_sem.at[1]),
        pltpu.make_async_copy(grads, grad_raw, load_sem.at[2]),
        pltpu.make_async_copy(dec, dec_all.at[down], load_sem.at[3]),
        pltpu.make_async_copy(upb_in, upb, load_sem.at[4]),
        pltpu.make_async_copy(deltas, del_raw, load_sem.at[5]),
    ]
    for copy in loads:
        copy.start()

    def remote(src, dst, kind, recv, dev):
        return pltpu.make_async_remote_copy(
            src, dst, send_sem.at[kind], recv, device_id=dev, device_id_type=MESH)

    def dec_half(r, i, owner):
        m = (i + r) % 2
        ref = dec_all.at[owner, m * part:(m + 1) * part]
        return remote(ref, ref, 0, dec_recv.at[r, i], ring_to[r])

    def dec_relay(r, i, owner):
        ref = dec_all.at[owner, r * part + i * piece:r * part + (i + 1) * piece]
        return remote(ref, ref, 0, dec_recv.at[r, 2 + i], ring_to[r])

    def enc_rows(level, c):
        return pl.ds(pl.multiple_of((level * 2 + c) * height, 16), height)

    def enc_a(level, c):
        return pl.ds(pl.multiple_of((level * 2 + c) * height + (1 - c) * TAIL, 16), height - TAIL)

    def enc_b(level, c):
        return pl.ds(pl.multiple_of((level * 2 + c) * height + c * (height - TAIL), 16), TAIL)

    def enc_copy(r, level, h, where, sem):
        ref = enc_all.at[h, where(level, core)]
        return remote(ref, ref, 1, enc_recv.at[sem], (up + 2 * step_of[r], down))

    def pair_copy(ref, sem):
        return remote(ref, ref, 2, pair_recv.at[sem], pair)

    def del_copy(dev):
        ref = del_all.at[down]
        return remote(ref, ref, 3, del_recv.at[0], dev)

    def grad_rows(level, c):
        return grad_all.at[pl.ds(pl.multiple_of((level * 2 + c) * toks, toks), toks)]

    def grad_copy(dev):
        ref = grad_rows(z, core)
        return remote(ref, ref, 4, grad_recv.at[0], dev)

    def pair_grad(level):
        ref = grad_rows(level, core)
        return remote(ref, ref, 5, grad_recv.at[1], pair)

    def pick_enc(h):
        for s in range(h * dact // 2, (h + 1) * dact // 2):
            at = s * BLOCK - h * half
            enc_all[h, pl.ds(pl.multiple_of(up * height, 16), height), at:at + BLOCK] = pick(
                enc_raw, slice(0, height), downb[s], blocks)

    loads[0].wait()
    loads[2].wait()
    for s in range(dact):
        grad_all[pl.ds(pl.multiple_of(up * toks, toks), toks), s * BLOCK:(s + 1) * BLOCK] = pick(
            grad_raw, slice(0, toks), downb[s], blocks)
    loads[1].wait()
    pick_enc(0)
    pl.semaphore_wait(barrier, len(others) + 1 + len(levels_of))

    def send_enc(h):
        for r in range(2):
            @pl.when(can_go[r])
            def _():
                enc_copy(r, z, h, enc_rows, 2 * z + h).start()

    for dev in levels_of:
        grad_copy(dev).start()
    send_enc(0)
    loads[3].wait()
    for i in range(2):
        for r in range(2):
            dec_half(r, i, down).start()
    pick_enc(1)
    send_enc(1)
    pair_copy(enc_all.at[:, enc_rows(z, core)], z).start()
    loads[4].wait()
    loads[5].wait()
    for w in range(wins):
        for s in range(uact):
            del_all[down, w, :, s * BLOCK:(s + 1) * BLOCK] = pick(
                del_raw, slice(w * win, (w + 1) * win), upb[s, down * wins + w], rows // BLOCK)
    for dev in others:
        del_copy(dev).start()

    acc[...] = jnp.zeros_like(acc)

    def mult(q, rs, n):
        acc[n, rs] += jnp.dot(
            dec_all[q, rs, :], enc_all[n, pl.ds(pl.multiple_of(q * depth, 128), depth), :],
            preferred_element_type=F32)

    def enc_stage(q, n):
        gap = jnp.maximum(q - z, z - q)
        return jnp.where(gap == last, 5 + n, 2 * gap)

    def products(low, high):
        @pl.loop(0, 4 * levels)
        def _(u):
            q, m, n = u // 4, u // 2 % 2, u % 2
            first = jnp.where(jnp.where(q == left, 1, 0) + m == 1, 2, 4)
            stage = jnp.maximum(enc_stage(q, n), jnp.where(q == down, 0, first))
            ready = jnp.logical_and(stage >= low, stage <= high)

            @pl.when(jnp.logical_and(ready, q != diag))
            def _():
                mult(q, pl.ds(pl.multiple_of(m * part, part), part), n)

    def diag_products(i):
        @pl.loop(0, 4)
        def _(u):
            m, n = u // 2, u % 2

            @pl.when(enc_stage(diag, n) <= 5)
            def _():
                mult(diag, pl.ds(pl.multiple_of(m * part + i * piece, piece), piece), n)

    def pair_whole(level):
        return pair_copy(enc_all.at[:, enc_rows(level, 1 - core)], level)

    def each(j, act):
        for r in range(2):
            level = z - step_of[r] * j

            @pl.when(inside(level))
            def _():
                act(r, level)

    def relay(j, h):
        def act(r, level):
            enc_copy(r, level, h, enc_rows, 2 * level + h).wait_recv()

            @pl.when(can_go[r])
            def _():
                if j == last - 1 and h == 1:
                    enc_copy(r, level, h, enc_a, 2 * level + h).start()
                    enc_copy(r, level, h, enc_b, 2 * levels).start()
                else:
                    enc_copy(r, level, h, enc_rows, 2 * level + h).start()
            if h == 1:
                pair_copy(enc_all.at[:, enc_rows(level, core)], level).start()
        each(j, act)

    relay(1, 0)
    pltpu.make_async_copy(
        grad_all.at[pl.ds(0, (levels - 1) * toks)], grad_all.at[pl.ds(0, (levels - 1) * toks)], grad_recv.at[0]).wait()
    for level in range(levels):
        pair_grad(level).start()
    relay(1, 1)
    for r in range(2):
        dec_half(r, 0, ring_from[r]).wait_recv()
        for i in range(2):
            dec_relay(r, i, ring_from[r]).start()
    pair_whole(z).wait_recv()
    each(1, lambda r, level: pair_whole(level).wait_recv())
    products(0, 2)
    relay(2, 0)

    pltpu.make_async_copy(
        del_all.at[pl.ds(0, n_down - 1)], del_all.at[pl.ds(0, n_down - 1)], del_recv.at[0]).wait()
    pltpu.make_async_copy(
        grad_all.at[pl.ds(0, levels * toks)], grad_all.at[pl.ds(0, levels * toks)], grad_recv.at[1]).wait()
    for d in range(n_down):
        for w in range(wins):
            for b in range(rows // BLOCK):
                value = jnp.zeros((win, BLOCK), masked.dtype)
                for s in range(uact):
                    on = flag(upb[s, d * wins + w], b, masked.dtype)
                    value = value + del_all[d, w, :, s * BLOCK:(s + 1) * BLOCK] * on
                t = (d * wins + w) * win
                masked[t:t + win, b * BLOCK:(b + 1) * BLOCK] = value
    prod[...] = lax.dot_general(
        masked[...], grad_all[...], (((0,), (0,)), ((), ())), preferred_element_type=F32)

    relay(2, 1)
    for r in range(2):
        dec_half(r, 1, ring_from[r]).wait_recv()
    each(2, lambda r, level: pair_whole(level).wait_recv())
    products(3, 4)

    far = last - z

    def end_wait(h, where, sem):
        for r in range(2):
            @pl.when(z == (0 if r else last))
            def _():
                enc_copy(r, far, h, where, sem).wait_recv()

    @pl.when(at_end)
    def _():
        end_wait(0, enc_rows, 2 * far)
        pair_copy(enc_all.at[0, enc_rows(far, core)], far).start()
    for r in range(2):
        dec_relay(r, 0, diag).wait_recv()

    @pl.when(at_end)
    def _():
        pair_copy(enc_all.at[0, enc_rows(far, 1 - core)], far).wait_recv()
    products(5, 5)
    diag_products(0)

    def mult_end(start, size):
        ks = pl.ds(pl.multiple_of(start, BLOCK), size)
        acc[1] += jnp.dot(
            dec_all[far, :, ks], enc_all[1, pl.ds(pl.multiple_of(far * depth + start, BLOCK), size), :],
            preferred_element_type=F32)

    @pl.when(at_end)
    def _():
        end_wait(1, enc_a, 2 * far + 1)
        pair_copy(enc_all.at[1, enc_a(far, core)], levels).start()
        end_wait(1, enc_b, 2 * levels)
        pair_copy(enc_all.at[1, enc_b(far, core)], levels + 1).start()
    for r in range(2):
        dec_relay(r, 1, diag).wait_recv()
    diag_products(1)

    @pl.when(at_end)
    def _():
        pair_copy(enc_all.at[1, enc_a(far, 1 - core)], levels).wait_recv()
        mult_end(TAIL, depth - 2 * TAIL)
        mult_end(core * (depth - TAIL), TAIL)
        pair_copy(enc_all.at[1, enc_b(far, 1 - core)], levels + 1).wait_recv()
        mult_end((1 - core) * (depth - TAIL), TAIL)

    tile = 64

    @pl.loop(0, rows // tile)
    def _(t):
        rs = pl.ds(pl.multiple_of(t * tile, tile), tile)
        values = []
        for s in range(dact):
            side, at = divmod(s * BLOCK, half)
            values.append(acc[side, rs, at:at + BLOCK] * prod[rs, s * BLOCK:(s + 1) * BLOCK])
        for c in range(blocks):
            total = None
            for s in range(dact):
                term = values[s] * flag(downb[s], c, F32)
                total = term if total is None else total + term
            out[rs, c * BLOCK:(c + 1) * BLOCK] = total

    def sent(ref, kind):
        pltpu.make_async_copy(ref, ref, send_sem.at[kind]).wait()

    sent(dec_all.at[pl.ds(0, 3)], 0)

    @pl.when(at_end)
    def _():
        sent(enc_all.at[:, pl.ds(0, height)], 1)

    @pl.when(jnp.logical_not(at_end))
    def _():
        sent(enc_all.at[:, pl.ds(0, (levels + 1) * height)], 1)
    sent(enc_all.at[:, pl.ds(0, levels * height)], 2)
    sent(del_all.at[pl.ds(0, n_down - 1)], 3)
    sent(grad_all.at[pl.ds(0, (levels - 1) * toks)], 4)
    sent(grad_all.at[pl.ds(0, levels * toks)], 5)


def ring_local(n_up, n_down, win, deltas, gradients, up_blocks, down_blocks, decoder, encoder):
    rows, depth = decoder.shape
    height, cols = encoder.shape
    toks = gradients.shape[0]
    uact, dact = up_blocks.shape[1], down_blocks.shape[0]
    tokens = deltas.shape[0] * n_down
    wins = deltas.shape[0] // win
    used = dact * BLOCK
    levels = n_up // 2
    kind = decoder.dtype
    dma = pltpu.SemaphoreType.DMA
    hbm = pl.BlockSpec(memory_space=pltpu.HBM)
    return pl.pallas_call(
        functools.partial(gather_scores, n_up, n_down),
        out_shape=jax.ShapeDtypeStruct((rows, cols), F32),
        in_specs=[hbm] * 6,
        out_specs=pl.BlockSpec(memory_space=pltpu.VMEM),
        scratch_shapes=[
            pltpu.SMEM((uact, up_blocks.shape[0]), jnp.int32),
            pltpu.SMEM((dact,), jnp.int32),
            pltpu.VMEM((n_down, rows, depth), kind),
            pltpu.VMEM((height, cols), kind),
            pltpu.VMEM((2, n_up * height, used // 2), kind),
            pltpu.VMEM(deltas.shape, kind),
            pltpu.VMEM((n_down, wins, win, uact * BLOCK), kind),
            pltpu.VMEM((toks, cols), kind),
            pltpu.VMEM((n_up * toks, used), kind),
            pltpu.VMEM((tokens, rows), kind),
            pltpu.VMEM((2, rows, used // 2), F32),
            pltpu.VMEM((rows, used), F32),
            dma((6,)),
            dma((6,)),
            dma((2, 4)),
            dma((1,)),
            dma((2 * levels + 1,)),
            dma((levels + 2,)),
            dma((2,)),
        ],
        compiler_params=pltpu.CompilerParams(collective_id=0, has_side_effects=True, vmem_limit_bytes=LARGE),
        name="gather_scores",
    )(*[pltpu.with_memory_space_constraint(x, pltpu.HBM) for x in (up_blocks.T, down_blocks, deltas, gradients, decoder, encoder)])


def plain_local(deltas, gradients, up_blocks, down_blocks, decoder, encoder):
    token_deltas = lax.all_gather(deltas, "down", axis=0, tiled=True)
    token_grads = lax.all_gather(gradients, "up", axis=0, tiled=True)
    tokens, rows = token_deltas.shape
    windows, dact = up_blocks.shape[0], down_blocks.shape[0]
    row_blocks, col_blocks = rows // BLOCK, encoder.shape[1] // BLOCK
    local_ids = jnp.arange(row_blocks, dtype=jnp.int32)
    block_on = jnp.any(up_blocks[:, :, None] == local_ids[None, None, :], axis=1)
    masked = token_deltas.reshape(windows, tokens // windows, row_blocks, BLOCK) * block_on[
        :, None, :, None].astype(token_deltas.dtype)
    masked = masked.reshape(tokens, rows)
    dec_whole = lax.all_gather(decoder, "down", axis=1, tiled=True)
    height = encoder.shape[0]
    enc_used = jnp.take(encoder.reshape(height, col_blocks, BLOCK), down_blocks, axis=1).reshape(height, dact * BLOCK)
    virtual = jnp.dot(dec_whole, lax.all_gather(enc_used, "up", axis=0, tiled=True), preferred_element_type=F32)
    grad_used = jnp.take(token_grads.reshape(tokens, col_blocks, BLOCK), down_blocks, axis=1).reshape(tokens, dact * BLOCK)
    product = lax.dot_general(masked, grad_used, (((0,), (0,)), ((), ())), preferred_element_type=F32)
    scored = (product * virtual).reshape(rows, dact, BLOCK)
    filled = jnp.zeros((rows, col_blocks, BLOCK), F32).at[:, down_blocks, :].set(scored)
    return filled.reshape(rows, encoder.shape[1])


def solution(mesh):
    n_up, n_down = mesh.shape["up"], mesh.shape["down"]
    ringed = n_down == 4 and n_up == 2 * n_down

    def local(deltas, gradients, up_blocks, down_blocks, decoder, encoder):
        args = (deltas, gradients, up_blocks, down_blocks, decoder, encoder)
        tokens = deltas.shape[0] * n_down
        win = tokens // up_blocks.shape[0]
        if ringed and deltas.shape[0] == 2 * win:
            return ring_local(n_up, n_down, win, *args)
        return plain_local(*args)

    placed = (P("down", "up"), P("up", "down"), P(None, "up"), P("down"), P("up", "down"), P("up", "down"))
    return jax.shard_map(local, mesh=mesh, in_specs=placed, out_specs=P("up", "down"), check_vma=False)
```

time: 52.6 us -> 50.1 us (0.952); the launches traced: 51.6 us -> 50 us
  Pallas kernels: 51.6 us -> 48.6 us
  local copies, waits for them, and re-layouts: 0 us -> 1.32 us
    pallas_call x1 -> x0, Pallas kernels: 2.2 us -> none  [ring_local(): pl.pallas_call(spread, out_shape=jax.ShapeDtypeStruct((rows, cols), F32),...]
    unnamed x0 -> x1, local copies, waits for them, and re-layouts: none -> 1.32 us
    pallas_call x1, Pallas kernels: 49.4 us -> 48.6 us  [ring_local(): pl.pallas_call(functools.partial(gather_scores, n_up, n_down), out_shape=...]
where the time goes in v1:
time: 50.1 us; the launch traced here: 50 us
  Pallas kernels  48.6 us (97%)
  local copies, waits for them, and re-layouts  1.32 us (3%)
    pallas_call x1, Pallas kernels, ring_local(): pl.pallas_call(functools.partial(gather_scores, n_up, n_down), out_shape=...  48.6 us
    unnamed x1, local copies, waits for them, and re-layouts  1.32 us

profile of v1, /device:TPU:0, one launch (start us, length us, event | category | flops | bytes accessed | tf_op | source)
XLA Modules:
  0.0 50.0 jit_solution(14982709818040520077)
XLA Ops:
  0.0 48.6 %gather_scores.1 = f32[512,1024]{1,0:T(8,128)S(1)} custom-call(s32[2,8]{1,0:T(2,128)} %bitcast.1, s32[4]{0:T(128)} %downb_in.1, bf16[64,512]{1,0:T(8,128)(2,1)} %deltas.1, bf16[32,1024]{1,0:T(8,128)(2,1)} %grads.1, bf16[512,1152]{1,0:T(8,128)(2,1)} %dec.1, bf16[576,1024]{1,0:T(8,128)(2,1)} %enc.1), custom_call_target="tpu_custom_call" | custom-call | tf_op jit(solution)/shard_map/gather_scores/pallas_call | solution.py:348
  48.6 1.3 %copy.8 = f32[512,1024]{1,0:T(8,128)} copy(f32[512,1024]{1,0:T(8,128)S(1)} %gather_scores.1) | data formatting | bytes 4194304

commit v2 on v1

--- a/solution.py
+++ b/solution.py
@@ -26,17 +26,25 @@
     return total
 
 
+def block(number):
+    return pl.ds(pl.multiple_of(number * BLOCK, BLOCK), BLOCK)
+
+
+def hits_of(number, slots):
+    return [1 - jnp.minimum(jnp.abs(slot - number), 1) for slot in slots]
+
+
 def gather_scores(
     n_up, n_down, upb_in, downb_in, deltas, grads, dec, enc, out,
     upb, downb, dec_all, enc_raw, enc_all, del_raw, del_all, grad_raw, grad_all, masked, acc, prod,
-    load_sem, send_sem, dec_recv, del_recv, enc_recv, pair_recv, grad_recv,
+    load_sem, send_sem, dec_recv, del_recv, enc_recv, pair_recv, grad_recv, pg_recv, ready,
 ):
     levels = n_up // 2
     rows, depth = dec.shape
     height = enc.shape[0]
     half = enc_all.shape[2]
     part = rows // 2
-    piece = part // 2
+    body = depth - TAIL
     toks = grads.shape[0]
     wins = del_all.shape[1]
     win = del_all.shape[2]
@@ -58,16 +66,26 @@
     last = levels - 1
     at_end = jnp.logical_or(z == 0, z == last)
     inside = lambda level: jnp.logical_and(level >= 0, level < levels)
-    levels_of = [(2 * ((z + i) % levels) + core, down) for i in range(1, levels)]
+    low, high = levels // 2 - 1, levels // 2
+    above = jnp.logical_and(z < last, z != low)
+    below = jnp.logical_and(z > 0, z != high)
 
     barrier = pltpu.get_barrier_semaphore()
-    for dev in (*others, pair, *levels_of):
+    for dev in (*others, pair):
         pl.semaphore_signal(barrier, inc=1, device_id=dev, device_id_type=MESH)
+
+    @pl.when(z < last)
+    def _():
+        pl.semaphore_signal(barrier, inc=1, device_id=(up + 2, down), device_id_type=MESH)
+
+    @pl.when(below)
+    def _():
+        pl.semaphore_signal(barrier, inc=1, device_id=(up - 2, down), device_id_type=MESH)
 
     loads = [
         pltpu.make_async_copy(downb_in, downb, load_sem.at[0]),
-        pltpu.make_async_copy(enc, enc_raw, load_sem.at[1]),
-        pltpu.make_async_copy(grads, grad_raw, load_sem.at[2]),
+        pltpu.make_async_copy(grads, grad_raw, load_sem.at[1]),
+        pltpu.make_async_copy(enc, enc_raw, load_sem.at[2]),
         pltpu.make_async_copy(dec, dec_all.at[down], load_sem.at[3]),
         pltpu.make_async_copy(upb_in, upb, load_sem.at[4]),
         pltpu.make_async_copy(deltas, del_raw, load_sem.at[5]),
@@ -85,7 +103,7 @@
         return remote(ref, ref, 0, dec_recv.at[r, i], ring_to[r])
 
     def dec_relay(r, i, owner):
-        ref = dec_all.at[owner, r * part + i * piece:r * part + (i + 1) * piece]
+        ref = dec_all.at[owner, r * part:(r + 1) * part, (body if i else 0):(depth if i else body)]
         return remote(ref, ref, 0, dec_recv.at[r, 2 + i], ring_to[r])
 
     def enc_rows(level, c):
@@ -111,44 +129,45 @@
     def grad_rows(level, c):
         return grad_all.at[pl.ds(pl.multiple_of((level * 2 + c) * toks, toks), toks)]
 
-    def grad_copy(dev):
-        ref = grad_rows(z, core)
-        return remote(ref, ref, 4, grad_recv.at[0], dev)
+    def grad_copy(r, level):
+        ref = grad_rows(level, core)
+        return remote(ref, ref, 4, grad_recv.at[level], (up + 2 * step_of[r], down))
 
     def pair_grad(level):
         ref = grad_rows(level, core)
-        return remote(ref, ref, 5, grad_recv.at[1], pair)
+        return remote(ref, ref, 5, pg_recv.at[0], pair)
 
     def pick_enc(h):
         for s in range(h * dact // 2, (h + 1) * dact // 2):
             at = s * BLOCK - h * half
-            enc_all[h, pl.ds(pl.multiple_of(up * height, 16), height), at:at + BLOCK] = pick(
-                enc_raw, slice(0, height), downb[s], blocks)
+            enc_all[h, pl.ds(pl.multiple_of(up * height, 16), height), at:at + BLOCK] = pick(enc_raw, slice(0, height), downb[s], blocks)
 
     loads[0].wait()
+    loads[1].wait()
+    for s in range(dact):
+        grad_all[pl.ds(pl.multiple_of(up * toks, toks), toks), s * BLOCK:(s + 1) * BLOCK] = pick(grad_raw, slice(0, toks), downb[s], blocks)
+    pl.semaphore_wait(barrier, len(others) + 1 + jnp.where(z > 0, 1, 0) + jnp.where(above, 1, 0))
+
+    @pl.when(z == high)
+    def _():
+        pl.semaphore_signal(ready, inc=1, device_id=(up - 2, down), device_id_type=MESH)
+
+    early = (above, z > 0)
+
+    def send_own(which, act):
+        for r in (1, 0):
+            @pl.when(which[r])
+            def _():
+                act(r)
+
+    send_own(early, lambda r: grad_copy(r, z).start())
     loads[2].wait()
-    for s in range(dact):
-        grad_all[pl.ds(pl.multiple_of(up * toks, toks), toks), s * BLOCK:(s + 1) * BLOCK] = pick(
-            grad_raw, slice(0, toks), downb[s], blocks)
-    loads[1].wait()
     pick_enc(0)
-    pl.semaphore_wait(barrier, len(others) + 1 + len(levels_of))
-
-    def send_enc(h):
-        for r in range(2):
-            @pl.when(can_go[r])
-            def _():
-                enc_copy(r, z, h, enc_rows, 2 * z + h).start()
-
-    for dev in levels_of:
-        grad_copy(dev).start()
-    send_enc(0)
+    send_own(early, lambda r: enc_copy(r, z, 0, enc_rows, 2 * z).start())
     loads[3].wait()
-    for i in range(2):
-        for r in range(2):
-            dec_half(r, i, down).start()
+    for r in range(2):
+        dec_half(r, 0, down).start()
     pick_enc(1)
-    send_enc(1)
     pair_copy(enc_all.at[:, enc_rows(z, core)], z).start()
     loads[4].wait()
     loads[5].wait()
@@ -158,12 +177,40 @@
                 del_raw, slice(w * win, (w + 1) * win), upb[s, down * wins + w], rows // BLOCK)
     for dev in others:
         del_copy(dev).start()
+    for r in range(2):
+        dec_half(r, 1, down).start()
+
+    def each(j, act):
+        for r in range(2):
+            level = z - step_of[r] * j
+
+            @pl.when(inside(level))
+            def _():
+                act(r, level)
+
+    def relay_grad(r, level):
+        grad_copy(r, level).wait_recv()
+
+        @pl.when(can_go[r])
+        def _():
+            grad_copy(r, level).start()
+        pair_grad(level).start()
+
+    @pl.when(z == low)
+    def _():
+        pl.semaphore_wait(ready, 1)
+        grad_copy(0, z).start()
+        enc_copy(0, z, 0, enc_rows, 2 * z).start()
+    pair_grad(z).start()
+    each(1, relay_grad)
+    send_own(can_go, lambda r: enc_copy(r, z, 1, enc_rows, 2 * z + 1).start())
 
     acc[...] = jnp.zeros_like(acc)
 
-    def mult(q, rs, n):
+    def mult(q, rs, n, start=0, size=depth):
+        ks = pl.ds(pl.multiple_of(start, BLOCK), size)
         acc[n, rs] += jnp.dot(
-            dec_all[q, rs, :], enc_all[n, pl.ds(pl.multiple_of(q * depth, 128), depth), :],
+            dec_all[q, rs, ks], enc_all[n, pl.ds(pl.multiple_of(q * depth + start, BLOCK), size), :],
             preferred_element_type=F32)
 
     def enc_stage(q, n):
@@ -182,25 +229,16 @@
             def _():
                 mult(q, pl.ds(pl.multiple_of(m * part, part), part), n)
 
+    everything = slice(0, rows)
+
     def diag_products(i):
-        @pl.loop(0, 4)
-        def _(u):
-            m, n = u // 2, u % 2
-
+        for n in range(2):
             @pl.when(enc_stage(diag, n) <= 5)
             def _():
-                mult(diag, pl.ds(pl.multiple_of(m * part + i * piece, piece), piece), n)
+                mult(diag, everything, n, body if i else 0, TAIL if i else body)
 
     def pair_whole(level):
         return pair_copy(enc_all.at[:, enc_rows(level, 1 - core)], level)
-
-    def each(j, act):
-        for r in range(2):
-            level = z - step_of[r] * j
-
-            @pl.when(inside(level))
-            def _():
-                act(r, level)
 
     def relay(j, h):
         def act(r, level):
@@ -218,10 +256,7 @@
         each(j, act)
 
     relay(1, 0)
-    pltpu.make_async_copy(
-        grad_all.at[pl.ds(0, (levels - 1) * toks)], grad_all.at[pl.ds(0, (levels - 1) * toks)], grad_recv.at[0]).wait()
-    for level in range(levels):
-        pair_grad(level).start()
+    each(2, relay_grad)
     relay(1, 1)
     for r in range(2):
         dec_half(r, 0, ring_from[r]).wait_recv()
@@ -230,12 +265,13 @@
     pair_whole(z).wait_recv()
     each(1, lambda r, level: pair_whole(level).wait_recv())
     products(0, 2)
+    each(3, relay_grad)
     relay(2, 0)
 
     pltpu.make_async_copy(
         del_all.at[pl.ds(0, n_down - 1)], del_all.at[pl.ds(0, n_down - 1)], del_recv.at[0]).wait()
     pltpu.make_async_copy(
-        grad_all.at[pl.ds(0, levels * toks)], grad_all.at[pl.ds(0, levels * toks)], grad_recv.at[1]).wait()
+        grad_all.at[pl.ds(0, levels * toks)], grad_all.at[pl.ds(0, levels * toks)], pg_recv.at[0]).wait()
     for d in range(n_down):
         for w in range(wins):
             for b in range(rows // BLOCK):
@@ -245,7 +281,8 @@
                     value = value + del_all[d, w, :, s * BLOCK:(s + 1) * BLOCK] * on
                 t = (d * wins + w) * win
                 masked[t:t + win, b * BLOCK:(b + 1) * BLOCK] = value
-    prod[...] = lax.dot_general(
+    prod[:, dact * BLOCK:] = jnp.zeros((rows, BLOCK), F32)
+    prod[:, :dact * BLOCK] = lax.dot_general(
         masked[...], grad_all[...], (((0,), (0,)), ((), ())), preferred_element_type=F32)
 
     relay(2, 1)
@@ -266,41 +303,34 @@
     def _():
         end_wait(0, enc_rows, 2 * far)
         pair_copy(enc_all.at[0, enc_rows(far, core)], far).start()
-    for r in range(2):
-        dec_relay(r, 0, diag).wait_recv()
-
-    @pl.when(at_end)
-    def _():
         pair_copy(enc_all.at[0, enc_rows(far, 1 - core)], far).wait_recv()
-    products(5, 5)
-    diag_products(0)
-
-    def mult_end(start, size):
-        ks = pl.ds(pl.multiple_of(start, BLOCK), size)
-        acc[1] += jnp.dot(
-            dec_all[far, :, ks], enc_all[1, pl.ds(pl.multiple_of(far * depth + start, BLOCK), size), :],
-            preferred_element_type=F32)
-
-    @pl.when(at_end)
-    def _():
+
+        @pl.when(far != diag)
+        def _():
+            mult(far, everything, 0)
         end_wait(1, enc_a, 2 * far + 1)
         pair_copy(enc_all.at[1, enc_a(far, core)], levels).start()
+    for r in range(2):
+        dec_relay(r, 0, diag).wait_recv()
+    diag_products(0)
+
+    @pl.when(at_end)
+    def _():
+        pair_copy(enc_all.at[1, enc_a(far, 1 - core)], levels).wait_recv()
+        mult(far, everything, 1, TAIL, depth - 2 * TAIL)
+    for r in range(2):
+        dec_relay(r, 1, diag).wait_recv()
+    diag_products(1)
+
+    @pl.when(at_end)
+    def _():
         end_wait(1, enc_b, 2 * levels)
         pair_copy(enc_all.at[1, enc_b(far, core)], levels + 1).start()
-    for r in range(2):
-        dec_relay(r, 1, diag).wait_recv()
-    diag_products(1)
-
-    @pl.when(at_end)
-    def _():
-        pair_copy(enc_all.at[1, enc_a(far, 1 - core)], levels).wait_recv()
-        mult_end(TAIL, depth - 2 * TAIL)
-        mult_end(core * (depth - TAIL), TAIL)
+        mult(far, everything, 1, core * body, TAIL)
         pair_copy(enc_all.at[1, enc_b(far, 1 - core)], levels + 1).wait_recv()
-        mult_end((1 - core) * (depth - TAIL), TAIL)
+        mult(far, everything, 1, (1 - core) * body, TAIL)
 
     tile = 64
-
     @pl.loop(0, rows // tile)
     def _(t):
         rs = pl.ds(pl.multiple_of(t * tile, tile), tile)
@@ -323,13 +353,14 @@
     @pl.when(at_end)
     def _():
         sent(enc_all.at[:, pl.ds(0, height)], 1)
+        sent(grad_all.at[pl.ds(0, toks)], 4)
 
     @pl.when(jnp.logical_not(at_end))
     def _():
         sent(enc_all.at[:, pl.ds(0, (levels + 1) * height)], 1)
+        sent(grad_all.at[pl.ds(0, (levels + 1) * toks)], 4)
     sent(enc_all.at[:, pl.ds(0, levels * height)], 2)
     sent(del_all.at[pl.ds(0, n_down - 1)], 3)
-    sent(grad_all.at[pl.ds(0, (levels - 1) * toks)], 4)
     sent(grad_all.at[pl.ds(0, levels * toks)], 5)
 
 
@@ -362,14 +393,16 @@
             pltpu.VMEM((n_up * toks, used), kind),
             pltpu.VMEM((tokens, rows), kind),
             pltpu.VMEM((2, rows, used // 2), F32),
-            pltpu.VMEM((rows, used), F32),
+            pltpu.VMEM((rows, used + BLOCK), F32),
             dma((6,)),
             dma((6,)),
             dma((2, 4)),
             dma((1,)),
             dma((2 * levels + 1,)),
             dma((levels + 2,)),
-            dma((2,)),
+            dma((levels,)),
+            dma((1,)),
+            pltpu.SemaphoreType.REGULAR,
         ],
         compiler_params=pltpu.CompilerParams(collective_id=0, has_side_effects=True, vmem_limit_bytes=LARGE),
         name="gather_scores",

time: 50.1 us -> 49.9 us (level)
  no operation moved by 1% of the time
where the time goes in v2:
time: 49.9 us; the launch traced here: 49.7 us
  Pallas kernels  48.4 us (97%)
  local copies, waits for them, and re-layouts  1.32 us (3%)
    pallas_call x1, Pallas kernels, ring_local(): pl.pallas_call(functools.partial(gather_scores, n_up, n_down), out_shape=...  48.4 us
    unnamed x1, local copies, waits for them, and re-layouts  1.32 us

profile of v2, /device:TPU:0, one launch (start us, length us, event | category | flops | bytes accessed | tf_op | source)
XLA Modules:
  0.0 49.7 jit_solution(12310175855713761005)
XLA Ops:
  0.0 48.4 %gather_scores.1 = f32[512,1024]{1,0:T(8,128)S(1)} custom-call(s32[2,8]{1,0:T(2,128)} %bitcast.1, s32[4]{0:T(128)} %downb_in.1, bf16[64,512]{1,0:T(8,128)(2,1)} %deltas.1, bf16[32,1024]{1,0:T(8,128)(2,1)} %grads.1, bf16[512,1152]{1,0:T(8,128)(2,1)} %dec.1, bf16[576,1024]{1,0:T(8,128)(2,1)} %enc.1), custom_call_target="tpu_custom_call" | custom-call | tf_op jit(solution)/shard_map/gather_scores/pallas_call | solution.py:379
  48.4 1.3 %copy.8 = f32[512,1024]{1,0:T(8,128)} copy(f32[512,1024]{1,0:T(8,128)S(1)} %gather_scores.1) | data formatting | bytes 4194304

commit v3 on v2

--- a/solution.py
+++ b/solution.py
@@ -37,7 +37,7 @@
 def gather_scores(
     n_up, n_down, upb_in, downb_in, deltas, grads, dec, enc, out,
     upb, downb, dec_all, enc_raw, enc_all, del_raw, del_all, grad_raw, grad_all, masked, acc, prod,
-    load_sem, send_sem, dec_recv, del_recv, enc_recv, pair_recv, grad_recv, pg_recv, ready,
+    load_sem, send_sem, dec_recv, del_recv, enc_recv, pair_recv, grad_recv, pg_recv, ready_z, ready_xy,
 ):
     levels = n_up // 2
     rows, depth = dec.shape
@@ -66,22 +66,21 @@
     last = levels - 1
     at_end = jnp.logical_or(z == 0, z == last)
     inside = lambda level: jnp.logical_and(level >= 0, level < levels)
-    low, high = levels // 2 - 1, levels // 2
-    above = jnp.logical_and(z < last, z != low)
-    below = jnp.logical_and(z > 0, z != high)
 
     barrier = pltpu.get_barrier_semaphore()
-    for dev in (*others, pair):
-        pl.semaphore_signal(barrier, inc=1, device_id=dev, device_id_type=MESH)
-
-    @pl.when(z < last)
-    def _():
-        pl.semaphore_signal(barrier, inc=1, device_id=(up + 2, down), device_id_type=MESH)
-
-    @pl.when(below)
-    def _():
-        pl.semaphore_signal(barrier, inc=1, device_id=(up - 2, down), device_id_type=MESH)
-
+    pl.semaphore_signal(barrier, inc=1, device_id=pair, device_id_type=MESH)
+
+    def greet(sem, toward):
+        for d in range(n_down):
+            @pl.when(d > down if toward > 0 else d < down)
+            def _():
+                pl.semaphore_signal(ready_xy if sem is None else sem, inc=1, device_id=(up, d), device_id_type=MESH)
+
+        @pl.when(z < last if toward > 0 else z > 0)
+        def _():
+            pl.semaphore_signal(ready_z if sem is None else sem, inc=1, device_id=(up + 2 * toward, down), device_id_type=MESH)
+
+    greet(barrier, 1)
     loads = [
         pltpu.make_async_copy(downb_in, downb, load_sem.at[0]),
         pltpu.make_async_copy(grads, grad_raw, load_sem.at[1]),
@@ -146,25 +145,29 @@
     loads[1].wait()
     for s in range(dact):
         grad_all[pl.ds(pl.multiple_of(up * toks, toks), toks), s * BLOCK:(s + 1) * BLOCK] = pick(grad_raw, slice(0, toks), downb[s], blocks)
-    pl.semaphore_wait(barrier, len(others) + 1 + jnp.where(z > 0, 1, 0) + jnp.where(above, 1, 0))
-
-    @pl.when(z == high)
-    def _():
-        pl.semaphore_signal(ready, inc=1, device_id=(up - 2, down), device_id_type=MESH)
-
-    early = (above, z > 0)
-
-    def send_own(which, act):
+    pl.semaphore_wait(barrier, 1 + down + jnp.where(z > 0, 1, 0))
+    greet(None, -1)
+
+    def send_own(act):
         for r in (1, 0):
-            @pl.when(which[r])
+            @pl.when(can_go[r])
             def _():
                 act(r)
 
-    send_own(early, lambda r: grad_copy(r, z).start())
+    @pl.when(z > 0)
+    def _():
+        grad_copy(1, z).start()
     loads[2].wait()
     pick_enc(0)
-    send_own(early, lambda r: enc_copy(r, z, 0, enc_rows, 2 * z).start())
+
+    @pl.when(z > 0)
+    def _():
+        enc_copy(1, z, 0, enc_rows, 2 * z).start()
     loads[3].wait()
+
+    @pl.when(down < n_down - 1)
+    def _():
+        pl.semaphore_wait(ready_xy, n_down - 1 - down)
     for r in range(2):
         dec_half(r, 0, down).start()
     pick_enc(1)
@@ -196,22 +199,24 @@
             grad_copy(r, level).start()
         pair_grad(level).start()
 
-    @pl.when(z == low)
-    def _():
-        pl.semaphore_wait(ready, 1)
+    @pl.when(z < last)
+    def _():
+        pl.semaphore_wait(ready_z, 1)
         grad_copy(0, z).start()
         enc_copy(0, z, 0, enc_rows, 2 * z).start()
     pair_grad(z).start()
     each(1, relay_grad)
-    send_own(can_go, lambda r: enc_copy(r, z, 1, enc_rows, 2 * z + 1).start())
+    send_own(lambda r: enc_copy(r, z, 1, enc_rows, 2 * z + 1).start())
 
     acc[...] = jnp.zeros_like(acc)
 
     def mult(q, rs, n, start=0, size=depth):
         ks = pl.ds(pl.multiple_of(start, BLOCK), size)
-        acc[n, rs] += jnp.dot(
+        result = jnp.dot(
             dec_all[q, rs, ks], enc_all[n, pl.ds(pl.multiple_of(q * depth + start, BLOCK), size), :],
             preferred_element_type=F32)
+        for i in range(half // BLOCK):
+            acc[n * (half // BLOCK) + i, rs] += result[:, i * BLOCK:(i + 1) * BLOCK]
 
     def enc_stage(q, n):
         gap = jnp.maximum(q - z, z - q)
@@ -281,9 +286,11 @@
                     value = value + del_all[d, w, :, s * BLOCK:(s + 1) * BLOCK] * on
                 t = (d * wins + w) * win
                 masked[t:t + win, b * BLOCK:(b + 1) * BLOCK] = value
-    prod[:, dact * BLOCK:] = jnp.zeros((rows, BLOCK), F32)
-    prod[:, :dact * BLOCK] = lax.dot_general(
+    whole = lax.dot_general(
         masked[...], grad_all[...], (((0,), (0,)), ((), ())), preferred_element_type=F32)
+    for s in range(dact):
+        prod[s] = whole[:, s * BLOCK:(s + 1) * BLOCK]
+    prod[dact] = jnp.zeros((rows, BLOCK), F32)
 
     relay(2, 1)
     for r in range(2):
@@ -331,19 +338,18 @@
         mult(far, everything, 1, (1 - core) * body, TAIL)
 
     tile = 64
+    places = []
+    for c in range(blocks):
+        hits = [1 - jnp.minimum(jnp.abs(downb[s] - c), 1) for s in range(dact)]
+        slot = sum(s * hit for s, hit in enumerate(hits))
+        factor = slot + dact * (1 - sum(hits))
+        places.append((jnp.maximum(jnp.minimum(slot, dact - 1), 0), jnp.maximum(jnp.minimum(factor, dact), 0)))
+
     @pl.loop(0, rows // tile)
     def _(t):
         rs = pl.ds(pl.multiple_of(t * tile, tile), tile)
-        values = []
-        for s in range(dact):
-            side, at = divmod(s * BLOCK, half)
-            values.append(acc[side, rs, at:at + BLOCK] * prod[rs, s * BLOCK:(s + 1) * BLOCK])
-        for c in range(blocks):
-            total = None
-            for s in range(dact):
-                term = values[s] * flag(downb[s], c, F32)
-                total = term if total is None else total + term
-            out[rs, c * BLOCK:(c + 1) * BLOCK] = total
+        for c, (slot, factor) in enumerate(places):
+            out[rs, c * BLOCK:(c + 1) * BLOCK] = acc[slot, rs] * prod[factor, rs]
 
     def sent(ref, kind):
         pltpu.make_async_copy(ref, ref, send_sem.at[kind]).wait()
@@ -392,8 +398,8 @@
             pltpu.VMEM((toks, cols), kind),
             pltpu.VMEM((n_up * toks, used), kind),
             pltpu.VMEM((tokens, rows), kind),
-            pltpu.VMEM((2, rows, used // 2), F32),
-            pltpu.VMEM((rows, used + BLOCK), F32),
+            pltpu.VMEM((dact, rows, BLOCK), F32),
+            pltpu.VMEM((dact + 1, rows, BLOCK), F32),
             dma((6,)),
             dma((6,)),
             dma((2, 4)),
@@ -402,6 +408,7 @@
             dma((levels + 2,)),
             dma((levels,)),
             dma((1,)),
+            pltpu.SemaphoreType.REGULAR,
             pltpu.SemaphoreType.REGULAR,
         ],
         compiler_params=pltpu.CompilerParams(collective_id=0, has_side_effects=True, vmem_limit_bytes=LARGE),

time: 49.9 us -> 48.9 us (0.980)
  Pallas kernels: 48.4 us -> 47 us
    pallas_call x1, Pallas kernels: 48.4 us -> 47 us  [ring_local(): pl.pallas_call(functools.partial(gather_scores, n_up, n_down), out_shape=...]
where the time goes in v3:
time: 48.9 us; the launch traced here: 48.3 us
  Pallas kernels  47 us (96%)
  local copies, waits for them, and re-layouts  1.32 us (3%)
    pallas_call x1, Pallas kernels, ring_local(): pl.pallas_call(functools.partial(gather_scores, n_up, n_down), out_shape=...  47 us
    unnamed x1, local copies, waits for them, and re-layouts  1.32 us

profile of v3, /device:TPU:0, one launch (start us, length us, event | category | flops | bytes accessed | tf_op | source)
XLA Modules:
  0.0 48.3 jit_solution(6021221945217572359)
XLA Ops:
  0.0 47.0 %gather_scores.1 = f32[512,1024]{1,0:T(8,128)S(1)} custom-call(s32[2,8]{1,0:T(2,128)} %bitcast.1, s32[4]{0:T(128)} %downb_in.1, bf16[64,512]{1,0:T(8,128)(2,1)} %deltas.1, bf16[32,1024]{1,0:T(8,128)(2,1)} %grads.1, bf16[512,1152]{1,0:T(8,128)(2,1)} %dec.1, bf16[576,1024]{1,0:T(8,128)(2,1)} %enc.1), custom_call_target="tpu_custom_call" | custom-call | tf_op jit(solution)/shard_map/gather_scores/pallas_call | solution.py:385
  47.0 1.3 %copy.8 = f32[512,1024]{1,0:T(8,128)} copy(f32[512,1024]{1,0:T(8,128)S(1)} %gather_scores.1) | data formatting | bytes 4194304

commit v4 on v3

--- a/solution.py
+++ b/solution.py
@@ -8,7 +8,7 @@
 from jax.sharding import PartitionSpec as P
 
 BLOCK = 128
-TAIL = 256
+TAIL = 128
 LARGE = 24 << 20
 MESH = pl.DeviceIdType.MESH
 F32 = jnp.float32
@@ -18,16 +18,8 @@
     return jnp.where(jnp.full((1, BLOCK), number, jnp.int32) == block, 1.0, 0.0).astype(kind)
 
 
-def pick(ref, rows, number, blocks):
-    total = None
-    for b in range(blocks):
-        term = ref[rows, b * BLOCK:(b + 1) * BLOCK] * flag(number, b, ref.dtype)
-        total = term if total is None else total + term
-    return total
-
-
-def block(number):
-    return pl.ds(pl.multiple_of(number * BLOCK, BLOCK), BLOCK)
+def within(number, count):
+    return jnp.maximum(jnp.minimum(number, count - 1), 0)
 
 
 def hits_of(number, slots):
@@ -46,9 +38,7 @@
     part = rows // 2
     body = depth - TAIL
     toks = grads.shape[0]
-    wins = del_all.shape[1]
-    win = del_all.shape[2]
-    uact = upb.shape[0]
+    wins, uact, win = del_all.shape[1:4]
     dact = downb.shape[0]
     blocks = enc.shape[1] // BLOCK
     up, down = lax.axis_index("up"), lax.axis_index("down")
@@ -61,35 +51,40 @@
     ring_from = (left, right)
     step_of = (1, -1)
     pair = (2 * z + 1 - core, down)
-    others = [(up, right), (up, left), (up, diag)]
     can_go = (z < levels - 1, z > 0)
     last = levels - 1
     at_end = jnp.logical_or(z == 0, z == last)
     inside = lambda level: jnp.logical_and(level >= 0, level < levels)
 
+    high = levels // 2
+    later = jnp.where(right > down, 1, 0) + jnp.where(left > down, 1, 0)
     barrier = pltpu.get_barrier_semaphore()
-    pl.semaphore_signal(barrier, inc=1, device_id=pair, device_id_type=MESH)
-
-    def greet(sem, toward):
-        for d in range(n_down):
-            @pl.when(d > down if toward > 0 else d < down)
-            def _():
-                pl.semaphore_signal(ready_xy if sem is None else sem, inc=1, device_id=(up, d), device_id_type=MESH)
-
-        @pl.when(z < last if toward > 0 else z > 0)
-        def _():
-            pl.semaphore_signal(ready_z if sem is None else sem, inc=1, device_id=(up + 2 * toward, down), device_id_type=MESH)
-
-    greet(barrier, 1)
-    loads = [
-        pltpu.make_async_copy(downb_in, downb, load_sem.at[0]),
-        pltpu.make_async_copy(grads, grad_raw, load_sem.at[1]),
-        pltpu.make_async_copy(enc, enc_raw, load_sem.at[2]),
-        pltpu.make_async_copy(dec, dec_all.at[down], load_sem.at[3]),
-        pltpu.make_async_copy(upb_in, upb, load_sem.at[4]),
-        pltpu.make_async_copy(deltas, del_raw, load_sem.at[5]),
-    ]
-    for copy in loads:
+
+    def signal(sem, dev, when=None):
+        if when is None:
+            pl.semaphore_signal(sem, inc=1, device_id=dev, device_id_type=MESH)
+        else:
+            pl.when(when)(lambda: pl.semaphore_signal(sem, inc=1, device_id=dev, device_id_type=MESH))
+
+    signal(barrier, pair)
+    signal(barrier, (up + 2, down), z < last)
+    signal(barrier, (up - 2, down), z > high)
+    for d in (right, left):
+        signal(barrier, (up, d), d > down)
+
+    def by_block(src, dst, sem):
+        return [pltpu.make_async_copy(src.at[:, b * BLOCK:(b + 1) * BLOCK], dst.at[b], sem) for b in range(dst.shape[0])]
+
+    def loaded(ref, sem):
+        pltpu.make_async_copy(ref, ref, sem).wait()
+
+    load_downb = pltpu.make_async_copy(downb_in, downb, load_sem.at[0])
+    load_upb = pltpu.make_async_copy(upb_in, upb, load_sem.at[4])
+    load_dec = pltpu.make_async_copy(dec, dec_all.at[down], load_sem.at[3])
+    for copy in (
+        load_downb, *by_block(grads, grad_raw, load_sem.at[1]), load_dec, *by_block(enc, enc_raw, load_sem.at[2]),
+        load_upb, *by_block(deltas, del_raw, load_sem.at[5]),
+    ):
         copy.start()
 
     def remote(src, dst, kind, recv, dev):
@@ -121,9 +116,13 @@
     def pair_copy(ref, sem):
         return remote(ref, ref, 2, pair_recv.at[sem], pair)
 
-    def del_copy(dev):
-        ref = del_all.at[down]
-        return remote(ref, ref, 3, del_recv.at[0], dev)
+    def del_copy(r, owner):
+        ref = del_all.at[owner]
+        return remote(ref, ref, 3, del_recv.at[r], ring_to[r])
+
+    def del_relay(r, owner):
+        ref = del_all.at[owner, r]
+        return remote(ref, ref, 3, del_recv.at[2], ring_to[r])
 
     def grad_rows(level, c):
         return grad_all.at[pl.ds(pl.multiple_of((level * 2 + c) * toks, toks), toks)]
@@ -139,47 +138,51 @@
     def pick_enc(h):
         for s in range(h * dact // 2, (h + 1) * dact // 2):
             at = s * BLOCK - h * half
-            enc_all[h, pl.ds(pl.multiple_of(up * height, 16), height), at:at + BLOCK] = pick(enc_raw, slice(0, height), downb[s], blocks)
-
-    loads[0].wait()
-    loads[1].wait()
+            enc_all[h, pl.ds(pl.multiple_of(up * height, 16), height), at:at + BLOCK] = enc_raw[chosen[s]]
+
+    load_downb.wait()
+    chosen = [within(downb[s], blocks) for s in range(dact)]
+    loaded(grad_raw, load_sem.at[1])
     for s in range(dact):
-        grad_all[pl.ds(pl.multiple_of(up * toks, toks), toks), s * BLOCK:(s + 1) * BLOCK] = pick(grad_raw, slice(0, toks), downb[s], blocks)
-    pl.semaphore_wait(barrier, 1 + down + jnp.where(z > 0, 1, 0))
-    greet(None, -1)
-
-    def send_own(act):
+        grad_all[pl.ds(pl.multiple_of(up * toks, toks), toks), s * BLOCK:(s + 1) * BLOCK] = grad_raw[chosen[s]]
+    pl.semaphore_wait(barrier, 3 - later + jnp.where(z > 0, 1, 0) + jnp.where(z >= high, 1, 0) - jnp.where(z == last, 1, 0))
+    signal(ready_z, (up - 2, down), jnp.logical_and(z > 0, z <= high))
+    for d in (right, left):
+        signal(ready_xy, (up, d), d < down)
+
+    early = (jnp.logical_and(z >= high, z < last), z > 0)
+
+    def send_own(which, act):
         for r in (1, 0):
-            @pl.when(can_go[r])
+            @pl.when(which[r])
             def _():
                 act(r)
 
-    @pl.when(z > 0)
-    def _():
-        grad_copy(1, z).start()
-    loads[2].wait()
+    send_own(early, lambda r: grad_copy(r, z).start())
+    load_dec.wait()
+
+    @pl.when(later == 0)
+    def _():
+        for r in range(2):
+            dec_half(r, 0, down).start()
+    loaded(enc_raw, load_sem.at[2])
     pick_enc(0)
-
-    @pl.when(z > 0)
-    def _():
-        enc_copy(1, z, 0, enc_rows, 2 * z).start()
-    loads[3].wait()
-
-    @pl.when(down < n_down - 1)
-    def _():
-        pl.semaphore_wait(ready_xy, n_down - 1 - down)
-    for r in range(2):
-        dec_half(r, 0, down).start()
+    send_own(early, lambda r: enc_copy(r, z, 0, enc_rows, 2 * z).start())
     pick_enc(1)
+
+    @pl.when(later > 0)
+    def _():
+        pl.semaphore_wait(ready_xy, later)
+        for r in range(2):
+            dec_half(r, 0, down).start()
     pair_copy(enc_all.at[:, enc_rows(z, core)], z).start()
-    loads[4].wait()
-    loads[5].wait()
+    load_upb.wait()
+    loaded(del_raw, load_sem.at[5])
     for w in range(wins):
         for s in range(uact):
-            del_all[down, w, :, s * BLOCK:(s + 1) * BLOCK] = pick(
-                del_raw, slice(w * win, (w + 1) * win), upb[s, down * wins + w], rows // BLOCK)
-    for dev in others:
-        del_copy(dev).start()
+            del_all[down, w, s] = del_raw[within(upb[s, down * wins + w], rows // BLOCK), w * win:(w + 1) * win]
+    for r in range(2):
+        del_copy(r, down).start()
     for r in range(2):
         dec_half(r, 1, down).start()
 
@@ -199,14 +202,14 @@
             grad_copy(r, level).start()
         pair_grad(level).start()
 
-    @pl.when(z < last)
+    @pl.when(z < high)
     def _():
         pl.semaphore_wait(ready_z, 1)
         grad_copy(0, z).start()
         enc_copy(0, z, 0, enc_rows, 2 * z).start()
     pair_grad(z).start()
     each(1, relay_grad)
-    send_own(lambda r: enc_copy(r, z, 1, enc_rows, 2 * z + 1).start())
+    send_own(can_go, lambda r: enc_copy(r, z, 1, enc_rows, 2 * z + 1).start())
 
     acc[...] = jnp.zeros_like(acc)
 
@@ -267,37 +270,36 @@
         dec_half(r, 0, ring_from[r]).wait_recv()
         for i in range(2):
             dec_relay(r, i, ring_from[r]).start()
+    for r in range(2):
+        del_copy(r, ring_from[r]).wait_recv()
+        del_relay(r, ring_from[r]).start()
     pair_whole(z).wait_recv()
     each(1, lambda r, level: pair_whole(level).wait_recv())
     products(0, 2)
     each(3, relay_grad)
     relay(2, 0)
 
-    pltpu.make_async_copy(
-        del_all.at[pl.ds(0, n_down - 1)], del_all.at[pl.ds(0, n_down - 1)], del_recv.at[0]).wait()
-    pltpu.make_async_copy(
-        grad_all.at[pl.ds(0, levels * toks)], grad_all.at[pl.ds(0, levels * toks)], pg_recv.at[0]).wait()
+    relay(2, 1)
+    for r in range(2):
+        dec_half(r, 1, ring_from[r]).wait_recv()
+    each(2, lambda r, level: pair_whole(level).wait_recv())
+    products(3, 4)
+
+    loaded(del_all.at[diag], del_recv.at[2])
+    loaded(grad_all.at[pl.ds(0, levels * toks)], pg_recv.at[0])
     for d in range(n_down):
         for w in range(wins):
             for b in range(rows // BLOCK):
-                value = jnp.zeros((win, BLOCK), masked.dtype)
-                for s in range(uact):
-                    on = flag(upb[s, d * wins + w], b, masked.dtype)
-                    value = value + del_all[d, w, :, s * BLOCK:(s + 1) * BLOCK] * on
+                hits = hits_of(b, [upb[s, d * wins + w] for s in range(uact)])
+                slot = within(sum(s * hit for s, hit in enumerate(hits)), uact)
                 t = (d * wins + w) * win
-                masked[t:t + win, b * BLOCK:(b + 1) * BLOCK] = value
+                masked[t:t + win, b * BLOCK:(b + 1) * BLOCK] = del_all[d, w, slot] * flag(sum(hits), 1, masked.dtype)
     whole = lax.dot_general(
         masked[...], grad_all[...], (((0,), (0,)), ((), ())), preferred_element_type=F32)
     for s in range(dact):
         prod[s] = whole[:, s * BLOCK:(s + 1) * BLOCK]
     prod[dact] = jnp.zeros((rows, BLOCK), F32)
 
-    relay(2, 1)
-    for r in range(2):
-        dec_half(r, 1, ring_from[r]).wait_recv()
-    each(2, lambda r, level: pair_whole(level).wait_recv())
-    products(3, 4)
-
     far = last - z
 
     def end_wait(h, where, sem):
@@ -323,6 +325,8 @@
 
     @pl.when(at_end)
     def _():
+        end_wait(1, enc_b, 2 * levels)
+        pair_copy(enc_all.at[1, enc_b(far, core)], levels + 1).start()
         pair_copy(enc_all.at[1, enc_a(far, 1 - core)], levels).wait_recv()
         mult(far, everything, 1, TAIL, depth - 2 * TAIL)
     for r in range(2):
@@ -331,8 +335,6 @@
 
     @pl.when(at_end)
     def _():
-        end_wait(1, enc_b, 2 * levels)
-        pair_copy(enc_all.at[1, enc_b(far, core)], levels + 1).start()
         mult(far, everything, 1, core * body, TAIL)
         pair_copy(enc_all.at[1, enc_b(far, 1 - core)], levels + 1).wait_recv()
         mult(far, everything, 1, (1 - core) * body, TAIL)
@@ -340,10 +342,9 @@
     tile = 64
     places = []
     for c in range(blocks):
-        hits = [1 - jnp.minimum(jnp.abs(downb[s] - c), 1) for s in range(dact)]
+        hits = hits_of(c, [downb[s] for s in range(dact)])
         slot = sum(s * hit for s, hit in enumerate(hits))
-        factor = slot + dact * (1 - sum(hits))
-        places.append((jnp.maximum(jnp.minimum(slot, dact - 1), 0), jnp.maximum(jnp.minimum(factor, dact), 0)))
+        places.append((within(slot, dact), within(slot + dact * (1 - sum(hits)), dact + 1)))
 
     @pl.loop(0, rows // tile)
     def _(t):
@@ -391,11 +392,11 @@
             pltpu.SMEM((uact, up_blocks.shape[0]), jnp.int32),
             pltpu.SMEM((dact,), jnp.int32),
             pltpu.VMEM((n_down, rows, depth), kind),
-            pltpu.VMEM((height, cols), kind),
+            pltpu.VMEM((cols // BLOCK, height, BLOCK), kind),
             pltpu.VMEM((2, n_up * height, used // 2), kind),
-            pltpu.VMEM(deltas.shape, kind),
-            pltpu.VMEM((n_down, wins, win, uact * BLOCK), kind),
-            pltpu.VMEM((toks, cols), kind),
+            pltpu.VMEM((rows // BLOCK, deltas.shape[0], BLOCK), kind),
+            pltpu.VMEM((n_down, wins, uact, win, BLOCK), kind),
+            pltpu.VMEM((cols // BLOCK, toks, BLOCK), kind),
             pltpu.VMEM((n_up * toks, used), kind),
             pltpu.VMEM((tokens, rows), kind),
             pltpu.VMEM((dact, rows, BLOCK), F32),
@@ -403,7 +404,7 @@
             dma((6,)),
             dma((6,)),
             dma((2, 4)),
-            dma((1,)),
+            dma((3,)),
             dma((2 * levels + 1,)),
             dma((levels + 2,)),
             dma((levels,)),

time: 48.9 us -> 51.2 us (1.047)
  Pallas kernels: 47 us -> 49.7 us
    pallas_call x1, Pallas kernels: 47 us -> 49.7 us  [ring_local(): pl.pallas_call(functools.partial(gather_scores, n_up, n_down), out_shape=...]
where the time goes in v4:
time: 51.2 us; the launch traced here: 51 us
  Pallas kernels  49.7 us (97%)
  local copies, waits for them, and re-layouts  1.32 us (3%)
    pallas_call x1, Pallas kernels, ring_local(): pl.pallas_call(functools.partial(gather_scores, n_up, n_down), out_shape=...  49.7 us
    unnamed x1, local copies, waits for them, and re-layouts  1.32 us

profile of v4, /device:TPU:0, one launch (start us, length us, event | category | flops | bytes accessed | tf_op | source)
XLA Modules:
  0.0 51.0 jit_solution(15806928611499683311)
XLA Ops:
  0.0 49.7 %gather_scores.1 = f32[512,1024]{1,0:T(8,128)S(1)} custom-call(s32[2,8]{1,0:T(2,128)} %bitcast.1, s32[4]{0:T(128)} %downb_in.1, bf16[64,512]{1,0:T(8,128)(2,1)} %deltas.1, bf16[32,1024]{1,0:T(8,128)(2,1)} %grads.1, bf16[512,1152]{1,0:T(8,128)(2,1)} %dec.1, bf16[576,1024]{1,0:T(8,128)(2,1)} %enc.1), custom_call_target="tpu_custom_call" | custom-call | tf_op jit(solution)/shard_map/gather_scores/pallas_call | solution.py:386
  49.7 1.3 %copy.8 = f32[512,1024]{1,0:T(8,128)} copy(f32[512,1024]{1,0:T(8,128)S(1)} %gather_scores.1) | data formatting | bytes 4194304

commit v5 on v4

--- a/solution.py
+++ b/solution.py
@@ -268,11 +268,10 @@
     relay(1, 1)
     for r in range(2):
         dec_half(r, 0, ring_from[r]).wait_recv()
+        del_copy(r, ring_from[r]).wait_recv()
+        del_relay(r, ring_from[r]).start()
         for i in range(2):
             dec_relay(r, i, ring_from[r]).start()
-    for r in range(2):
-        del_copy(r, ring_from[r]).wait_recv()
-        del_relay(r, ring_from[r]).start()
     pair_whole(z).wait_recv()
     each(1, lambda r, level: pair_whole(level).wait_recv())
     products(0, 2)

time: 51.2 us -> 48.7 us (0.951)
  Pallas kernels: 49.7 us -> 47.1 us
    pallas_call x1, Pallas kernels: 49.7 us -> 47.1 us  [ring_local(): pl.pallas_call(functools.partial(gather_scores, n_up, n_down), out_shape=...]
where the time goes in v5:
time: 48.7 us; the launch traced here: 48.4 us
  Pallas kernels  47.1 us (97%)
  local copies, waits for them, and re-layouts  1.32 us (3%)
    pallas_call x1, Pallas kernels, ring_local(): pl.pallas_call(functools.partial(gather_scores, n_up, n_down), out_shape=...  47.1 us
    unnamed x1, local copies, waits for them, and re-layouts  1.32 us

profile of v5, /device:TPU:0, one launch (start us, length us, event | category | flops | bytes accessed | tf_op | source)
XLA Modules:
  0.0 48.4 jit_solution(8464395538541402552)
XLA Ops:
  0.0 47.1 %gather_scores.1 = f32[512,1024]{1,0:T(8,128)S(1)} custom-call(s32[2,8]{1,0:T(2,128)} %bitcast.1, s32[4]{0:T(128)} %downb_in.1, bf16[64,512]{1,0:T(8,128)(2,1)} %deltas.1, bf16[32,1024]{1,0:T(8,128)(2,1)} %grads.1, bf16[512,1152]{1,0:T(8,128)(2,1)} %dec.1, bf16[576,1024]{1,0:T(8,128)(2,1)} %enc.1), custom_call_target="tpu_custom_call" | custom-call | tf_op jit(solution)/shard_map/gather_scores/pallas_call | solution.py:385
  47.1 1.3 %copy.8 = f32[512,1024]{1,0:T(8,128)} copy(f32[512,1024]{1,0:T(8,128)S(1)} %gather_scores.1) | data formatting | bytes 4194304

commit v6 on v5

--- a/solution.py
+++ b/solution.py
@@ -8,7 +8,8 @@
 from jax.sharding import PartitionSpec as P
 
 BLOCK = 128
-TAIL = 128
+TAIL = 64
+LAST = 128
 LARGE = 24 << 20
 MESH = pl.DeviceIdType.MESH
 F32 = jnp.float32
@@ -36,7 +37,7 @@
     height = enc.shape[0]
     half = enc_all.shape[2]
     part = rows // 2
-    body = depth - TAIL
+    body = depth - LAST
     toks = grads.shape[0]
     wins, uact, win = del_all.shape[1:4]
     dact = downb.shape[0]
@@ -69,6 +70,8 @@
     signal(barrier, pair)
     signal(barrier, (up + 2, down), z < last)
     signal(barrier, (up - 2, down), z > high)
+    signal(barrier, (up + 3 - 2 * core, down), z == 0)
+    signal(barrier, (up - 1 - 2 * core, down), z == last)
     for d in (right, left):
         signal(barrier, (up, d), d > down)
 
@@ -94,35 +97,36 @@
     def dec_half(r, i, owner):
         m = (i + r) % 2
         ref = dec_all.at[owner, m * part:(m + 1) * part]
-        return remote(ref, ref, 0, dec_recv.at[r, i], ring_to[r])
+        return remote(ref, ref, 0, dec_recv.at[i], ring_to[r])
 
     def dec_relay(r, i, owner):
         ref = dec_all.at[owner, r * part:(r + 1) * part, (body if i else 0):(depth if i else body)]
-        return remote(ref, ref, 0, dec_recv.at[r, 2 + i], ring_to[r])
+        return remote(ref, ref, 0, dec_recv.at[2 + i], ring_to[r])
 
     def enc_rows(level, c):
         return pl.ds(pl.multiple_of((level * 2 + c) * height, 16), height)
 
     def enc_a(level, c):
-        return pl.ds(pl.multiple_of((level * 2 + c) * height + (1 - c) * TAIL, 16), height - TAIL)
+        return pl.ds(pl.multiple_of((level * 2 + c) * height + c * TAIL, 16), height - TAIL)
 
     def enc_b(level, c):
-        return pl.ds(pl.multiple_of((level * 2 + c) * height + c * (height - TAIL), 16), TAIL)
-
-    def enc_copy(r, level, h, where, sem):
+        return pl.ds(pl.multiple_of((level * 2 + c) * height + (1 - c) * (height - TAIL), 16), TAIL)
+
+    def enc_copy(r, level, h, where, sem, cross=False):
         ref = enc_all.at[h, where(level, core)]
-        return remote(ref, ref, 1, enc_recv.at[sem], (up + 2 * step_of[r], down))
+        target = up + 2 * step_of[r]
+        return remote(ref, ref, 1, enc_recv.at[sem], (target + 1 - 2 * core if cross else target, down))
 
     def pair_copy(ref, sem):
         return remote(ref, ref, 2, pair_recv.at[sem], pair)
 
     def del_copy(r, owner):
         ref = del_all.at[owner]
-        return remote(ref, ref, 3, del_recv.at[r], ring_to[r])
+        return remote(ref, ref, 3, del_recv.at[0], ring_to[r])
 
     def del_relay(r, owner):
         ref = del_all.at[owner, r]
-        return remote(ref, ref, 3, del_recv.at[2], ring_to[r])
+        return remote(ref, ref, 3, del_recv.at[1], ring_to[r])
 
     def grad_rows(level, c):
         return grad_all.at[pl.ds(pl.multiple_of((level * 2 + c) * toks, toks), toks)]
@@ -145,7 +149,9 @@
     loaded(grad_raw, load_sem.at[1])
     for s in range(dact):
         grad_all[pl.ds(pl.multiple_of(up * toks, toks), toks), s * BLOCK:(s + 1) * BLOCK] = grad_raw[chosen[s]]
-    pl.semaphore_wait(barrier, 3 - later + jnp.where(z > 0, 1, 0) + jnp.where(z >= high, 1, 0) - jnp.where(z == last, 1, 0))
+    pl.semaphore_wait(barrier, (
+        3 - later + jnp.where(z > 0, 1, 0) + jnp.where(z >= high, 1, 0) - jnp.where(z == last, 1, 0)
+        + jnp.where(z == 1, 1, 0) + jnp.where(z == last - 1, 1, 0)))
     signal(ready_z, (up - 2, down), jnp.logical_and(z > 0, z <= high))
     for d in (right, left):
         signal(ready_xy, (up, d), d < down)
@@ -243,7 +249,7 @@
         for n in range(2):
             @pl.when(enc_stage(diag, n) <= 5)
             def _():
-                mult(diag, everything, n, body if i else 0, TAIL if i else body)
+                mult(diag, everything, n, body if i else 0, LAST if i else body)
 
     def pair_whole(level):
         return pair_copy(enc_all.at[:, enc_rows(level, 1 - core)], level)
@@ -256,7 +262,8 @@
             def _():
                 if j == last - 1 and h == 1:
                     enc_copy(r, level, h, enc_a, 2 * level + h).start()
-                    enc_copy(r, level, h, enc_b, 2 * levels).start()
+                    for cross in (False, True):
+                        enc_copy(r, level, h, enc_b, 2 * levels, cross).start()
                 else:
                     enc_copy(r, level, h, enc_rows, 2 * level + h).start()
             if h == 1:
@@ -266,9 +273,9 @@
     relay(1, 0)
     each(2, relay_grad)
     relay(1, 1)
+    loaded(dec_all.at[left], dec_recv.at[0])
+    loaded(del_all.at[pl.ds(0, 2)], del_recv.at[0])
     for r in range(2):
-        dec_half(r, 0, ring_from[r]).wait_recv()
-        del_copy(r, ring_from[r]).wait_recv()
         del_relay(r, ring_from[r]).start()
         for i in range(2):
             dec_relay(r, i, ring_from[r]).start()
@@ -279,12 +286,11 @@
     relay(2, 0)
 
     relay(2, 1)
-    for r in range(2):
-        dec_half(r, 1, ring_from[r]).wait_recv()
+    loaded(dec_all.at[left], dec_recv.at[1])
     each(2, lambda r, level: pair_whole(level).wait_recv())
     products(3, 4)
 
-    loaded(del_all.at[diag], del_recv.at[2])
+    loaded(del_all.at[diag], del_recv.at[1])
     loaded(grad_all.at[pl.ds(0, levels * toks)], pg_recv.at[0])
     for d in range(n_down):
         for w in range(wins):
@@ -318,25 +324,30 @@
             mult(far, everything, 0)
         end_wait(1, enc_a, 2 * far + 1)
         pair_copy(enc_all.at[1, enc_a(far, core)], levels).start()
-    for r in range(2):
-        dec_relay(r, 0, diag).wait_recv()
+    loaded(dec_all.at[diag, :, :body], dec_recv.at[2])
     diag_products(0)
 
+    side = height - TAIL
+
+    def other_side():
+        pair_copy(enc_all.at[1, enc_a(far, 1 - core)], levels).wait_recv()
+        mult(far, everything, 1, (1 - core) * (depth - side), side)
+
+    def own_side():
+        mult(far, everything, 1, core * (depth - side), side)
+
+    soon = jnp.logical_or(core == 0, far != diag)
+    pl.when(jnp.logical_and(at_end, soon))(own_side)
+    loaded(dec_all.at[diag, :, body:], dec_recv.at[3])
+    pl.when(jnp.logical_and(at_end, jnp.logical_not(soon)))(own_side)
+    pl.when(jnp.logical_and(at_end, core == 0))(other_side)
+    diag_products(1)
+
     @pl.when(at_end)
     def _():
-        end_wait(1, enc_b, 2 * levels)
-        pair_copy(enc_all.at[1, enc_b(far, core)], levels + 1).start()
-        pair_copy(enc_all.at[1, enc_a(far, 1 - core)], levels).wait_recv()
-        mult(far, everything, 1, TAIL, depth - 2 * TAIL)
-    for r in range(2):
-        dec_relay(r, 1, diag).wait_recv()
-    diag_products(1)
-
-    @pl.when(at_end)
-    def _():
-        mult(far, everything, 1, core * body, TAIL)
-        pair_copy(enc_all.at[1, enc_b(far, 1 - core)], levels + 1).wait_recv()
-        mult(far, everything, 1, (1 - core) * body, TAIL)
+        loaded(enc_all.at[1, pl.ds(pl.multiple_of(far * depth + side, BLOCK), 2 * TAIL)], enc_recv.at[2 * levels])
+        mult(far, everything, 1, side, 2 * TAIL)
+        pl.when(core == 1)(other_side)
 
     tile = 64
     places = []
@@ -359,13 +370,14 @@
     @pl.when(at_end)
     def _():
         sent(enc_all.at[:, pl.ds(0, height)], 1)
+        sent(enc_all.at[:, pl.ds(0, levels * height - TAIL // 2)], 2)
         sent(grad_all.at[pl.ds(0, toks)], 4)
 
     @pl.when(jnp.logical_not(at_end))
     def _():
-        sent(enc_all.at[:, pl.ds(0, (levels + 1) * height)], 1)
+        sent(enc_all.at[:, pl.ds(0, (levels + 1) * height + TAIL // 2)], 1)
+        sent(enc_all.at[:, pl.ds(0, levels * height)], 2)
         sent(grad_all.at[pl.ds(0, (levels + 1) * toks)], 4)
-    sent(enc_all.at[:, pl.ds(0, levels * height)], 2)
     sent(del_all.at[pl.ds(0, n_down - 1)], 3)
     sent(grad_all.at[pl.ds(0, levels * toks)], 5)
 
@@ -402,10 +414,10 @@
             pltpu.VMEM((dact + 1, rows, BLOCK), F32),
             dma((6,)),
             dma((6,)),
-            dma((2, 4)),
-            dma((3,)),
+            dma((4,)),
+            dma((2,)),
             dma((2 * levels + 1,)),
-            dma((levels + 2,)),
+            dma((levels + 1,)),
             dma((levels,)),
             dma((1,)),
             pltpu.SemaphoreType.REGULAR,

time: 48.7 us -> 48.7 us (level)
  no operation moved by 1% of the time
where the time goes in v6:
time: 48.7 us; the launch traced here: 48.5 us
  Pallas kernels  47.2 us (97%)
  local copies, waits for them, and re-layouts  1.32 us (3%)
    pallas_call x1, Pallas kernels, ring_local(): pl.pallas_call(functools.partial(gather_scores, n_up, n_down), out_shape=...  47.2 us
    unnamed x1, local copies, waits for them, and re-layouts  1.32 us

profile of v6, /device:TPU:0, one launch (start us, length us, event | category | flops | bytes accessed | tf_op | source)
XLA Modules:
  0.0 48.5 jit_solution(9041864404045409193)
XLA Ops:
  0.0 47.2 %gather_scores.1 = f32[512,1024]{1,0:T(8,128)S(1)} custom-call(s32[2,8]{1,0:T(2,128)} %bitcast.1, s32[4]{0:T(128)} %downb_in.1, bf16[64,512]{1,0:T(8,128)(2,1)} %deltas.1, bf16[32,1024]{1,0:T(8,128)(2,1)} %grads.1, bf16[512,1152]{1,0:T(8,128)(2,1)} %dec.1, bf16[576,1024]{1,0:T(8,128)(2,1)} %enc.1), custom_call_target="tpu_custom_call" | custom-call | tf_op jit(solution)/shard_map/gather_scores/pallas_call | solution.py:397
  47.2 1.3 %copy.8 = f32[512,1024]{1,0:T(8,128)} copy(f32[512,1024]{1,0:T(8,128)S(1)} %gather_scores.1) | data formatting | bytes 4194304

commit v7 on v5

--- a/solution.py
+++ b/solution.py
@@ -94,11 +94,11 @@
     def dec_half(r, i, owner):
         m = (i + r) % 2
         ref = dec_all.at[owner, m * part:(m + 1) * part]
-        return remote(ref, ref, 0, dec_recv.at[r, i], ring_to[r])
+        return remote(ref, ref, 0, dec_recv.at[i], ring_to[r])
 
     def dec_relay(r, i, owner):
         ref = dec_all.at[owner, r * part:(r + 1) * part, (body if i else 0):(depth if i else body)]
-        return remote(ref, ref, 0, dec_recv.at[r, 2 + i], ring_to[r])
+        return remote(ref, ref, 0, dec_recv.at[2 + i], ring_to[r])
 
     def enc_rows(level, c):
         return pl.ds(pl.multiple_of((level * 2 + c) * height, 16), height)
@@ -118,11 +118,11 @@
 
     def del_copy(r, owner):
         ref = del_all.at[owner]
-        return remote(ref, ref, 3, del_recv.at[r], ring_to[r])
+        return remote(ref, ref, 3, del_recv.at[0], ring_to[r])
 
     def del_relay(r, owner):
         ref = del_all.at[owner, r]
-        return remote(ref, ref, 3, del_recv.at[2], ring_to[r])
+        return remote(ref, ref, 3, del_recv.at[1], ring_to[r])
 
     def grad_rows(level, c):
         return grad_all.at[pl.ds(pl.multiple_of((level * 2 + c) * toks, toks), toks)]
@@ -266,9 +266,9 @@
     relay(1, 0)
     each(2, relay_grad)
     relay(1, 1)
+    loaded(dec_all.at[left], dec_recv.at[0])
+    loaded(del_all.at[pl.ds(0, 2)], del_recv.at[0])
     for r in range(2):
-        dec_half(r, 0, ring_from[r]).wait_recv()
-        del_copy(r, ring_from[r]).wait_recv()
         del_relay(r, ring_from[r]).start()
         for i in range(2):
             dec_relay(r, i, ring_from[r]).start()
@@ -279,12 +279,11 @@
     relay(2, 0)
 
     relay(2, 1)
-    for r in range(2):
-        dec_half(r, 1, ring_from[r]).wait_recv()
+    loaded(dec_all.at[left], dec_recv.at[1])
     each(2, lambda r, level: pair_whole(level).wait_recv())
     products(3, 4)
 
-    loaded(del_all.at[diag], del_recv.at[2])
+    loaded(del_all.at[diag], del_recv.at[1])
     loaded(grad_all.at[pl.ds(0, levels * toks)], pg_recv.at[0])
     for d in range(n_down):
         for w in range(wins):
@@ -316,27 +315,33 @@
         @pl.when(far != diag)
         def _():
             mult(far, everything, 0)
+
+    def first_relay():
+        loaded(dec_all.at[diag, :, :body], dec_recv.at[2])
+        diag_products(0)
+
+    def inner():
+        pair_copy(enc_all.at[1, enc_a(far, 1 - core)], levels).wait_recv()
+        mult(far, everything, 1, core * TAIL, depth - TAIL)
+
+    @pl.when(at_end)
+    def _():
+        pl.when(core == 1)(first_relay)
         end_wait(1, enc_a, 2 * far + 1)
         pair_copy(enc_all.at[1, enc_a(far, core)], levels).start()
-    for r in range(2):
-        dec_relay(r, 0, diag).wait_recv()
-    diag_products(0)
-
-    @pl.when(at_end)
-    def _():
+        pl.when(core == 0)(first_relay)
         end_wait(1, enc_b, 2 * levels)
         pair_copy(enc_all.at[1, enc_b(far, core)], levels + 1).start()
-        pair_copy(enc_all.at[1, enc_a(far, 1 - core)], levels).wait_recv()
-        mult(far, everything, 1, TAIL, depth - 2 * TAIL)
-    for r in range(2):
-        dec_relay(r, 1, diag).wait_recv()
+        pl.when(core == 0)(inner)
+    pl.when(jnp.logical_not(at_end))(first_relay)
+    loaded(dec_all.at[diag, :, body:], dec_recv.at[3])
     diag_products(1)
 
     @pl.when(at_end)
     def _():
-        mult(far, everything, 1, core * body, TAIL)
+        pl.when(core == 1)(inner)
         pair_copy(enc_all.at[1, enc_b(far, 1 - core)], levels + 1).wait_recv()
-        mult(far, everything, 1, (1 - core) * body, TAIL)
+        mult(far, everything, 1, (1 - core) * (depth - TAIL), TAIL)
 
     tile = 64
     places = []
@@ -402,8 +407,8 @@
             pltpu.VMEM((dact + 1, rows, BLOCK), F32),
             dma((6,)),
             dma((6,)),
-            dma((2, 4)),
-            dma((3,)),
+            dma((4,)),
+            dma((2,)),
             dma((2 * levels + 1,)),
             dma((levels + 2,)),
             dma((levels,)),

time: 48.7 us -> 48.2 us (0.990)
  no operation moved by 1% of the time
where the time goes in v7:
time: 48.2 us; the launch traced here: 48 us
  Pallas kernels  46.7 us (97%)
  local copies, waits for them, and re-layouts  1.32 us (3%)
    pallas_call x1, Pallas kernels, ring_local(): pl.pallas_call(functools.partial(gather_scores, n_up, n_down), out_shape=...  46.7 us
    unnamed x1, local copies, waits for them, and re-layouts  1.32 us

profile of v7, /device:TPU:0, one launch (start us, length us, event | category | flops | bytes accessed | tf_op | source)
XLA Modules:
  0.0 48.0 jit_solution(11830420517519135766)
XLA Ops:
  0.0 46.7 %gather_scores.1 = f32[512,1024]{1,0:T(8,128)S(1)} custom-call(s32[2,8]{1,0:T(2,128)} %bitcast.1, s32[4]{0:T(128)} %downb_in.1, bf16[64,512]{1,0:T(8,128)(2,1)} %deltas.1, bf16[32,1024]{1,0:T(8,128)(2,1)} %grads.1, bf16[512,1152]{1,0:T(8,128)(2,1)} %dec.1, bf16[576,1024]{1,0:T(8,128)(2,1)} %enc.1), custom_call_target="tpu_custom_call" | custom-call | tf_op jit(solution)/shard_map/gather_scores/pallas_call | solution.py:390
  46.7 1.3 %copy.8 = f32[512,1024]{1,0:T(8,128)} copy(f32[512,1024]{1,0:T(8,128)S(1)} %gather_scores.1) | data formatting | bytes 4194304

commit v8 on v7

--- a/solution.py
+++ b/solution.py
@@ -82,7 +82,7 @@
     load_upb = pltpu.make_async_copy(upb_in, upb, load_sem.at[4])
     load_dec = pltpu.make_async_copy(dec, dec_all.at[down], load_sem.at[3])
     for copy in (
-        load_downb, *by_block(grads, grad_raw, load_sem.at[1]), load_dec, *by_block(enc, enc_raw, load_sem.at[2]),
+        load_downb, *by_block(grads, grad_raw, load_sem.at[1]), *by_block(enc, enc_raw, load_sem.at[2]), load_dec,
         load_upb, *by_block(deltas, del_raw, load_sem.at[5]),
     ):
         copy.start()
@@ -159,22 +159,24 @@
                 act(r)
 
     send_own(early, lambda r: grad_copy(r, z).start())
-    load_dec.wait()
-
-    @pl.when(later == 0)
-    def _():
-        for r in range(2):
-            dec_half(r, 0, down).start()
     loaded(enc_raw, load_sem.at[2])
     pick_enc(0)
     send_own(early, lambda r: enc_copy(r, z, 0, enc_rows, 2 * z).start())
+    load_dec.wait()
+
+    for r, d in enumerate((right, left)):
+        @pl.when(d < down)
+        def _():
+            dec_half(r, 0, down).start()
     pick_enc(1)
 
     @pl.when(later > 0)
     def _():
         pl.semaphore_wait(ready_xy, later)
-        for r in range(2):
-            dec_half(r, 0, down).start()
+        for r, d in enumerate((right, left)):
+            @pl.when(d > down)
+            def _():
+                dec_half(r, 0, down).start()
     pair_copy(enc_all.at[:, enc_rows(z, core)], z).start()
     load_upb.wait()
     loaded(del_raw, load_sem.at[5])

time: 48.2 us -> 48.1 us (level)
  no operation moved by 1% of the time
where the time goes in v8:
time: 48.1 us; the launch traced here: 47.9 us
  Pallas kernels  46.6 us (97%)
  local copies, waits for them, and re-layouts  1.32 us (3%)
    pallas_call x1, Pallas kernels, ring_local(): pl.pallas_call(functools.partial(gather_scores, n_up, n_down), out_shape=...  46.6 us
    unnamed x1, local copies, waits for them, and re-layouts  1.32 us

profile of v8, /device:TPU:0, one launch (start us, length us, event | category | flops | bytes accessed | tf_op | source)
XLA Modules:
  0.0 47.9 jit_solution(6532590171077348708)
XLA Ops:
  0.0 46.6 %gather_scores.1 = f32[512,1024]{1,0:T(8,128)S(1)} custom-call(s32[2,8]{1,0:T(2,128)} %bitcast.1, s32[4]{0:T(128)} %downb_in.1, bf16[64,512]{1,0:T(8,128)(2,1)} %deltas.1, bf16[32,1024]{1,0:T(8,128)(2,1)} %grads.1, bf16[512,1152]{1,0:T(8,128)(2,1)} %dec.1, bf16[576,1024]{1,0:T(8,128)(2,1)} %enc.1), custom_call_target="tpu_custom_call" | custom-call | tf_op jit(solution)/shard_map/gather_scores/pallas_call | solution.py:392
  46.6 1.3 %copy.8 = f32[512,1024]{1,0:T(8,128)} copy(f32[512,1024]{1,0:T(8,128)S(1)} %gather_scores.1) | data formatting | bytes 4194304

commit v9 on v8

--- a/solution.py
+++ b/solution.py
@@ -9,7 +9,7 @@
 
 BLOCK = 128
 TAIL = 128
-LARGE = 24 << 20
+LARGE, SMALL = 24 << 20, 8 << 20
 MESH = pl.DeviceIdType.MESH
 F32 = jnp.float32
 
@@ -27,8 +27,8 @@
 
 
 def gather_scores(
-    n_up, n_down, upb_in, downb_in, deltas, grads, dec, enc, out,
-    upb, downb, dec_all, enc_raw, enc_all, del_raw, del_all, grad_raw, grad_all, masked, acc, prod,
+    n_up, n_down, upb_in, downb_in, deltas, grads, dec, enc, acc, prod, table,
+    upb, downb, dec_all, enc_raw, enc_all, del_raw, del_all, grad_raw, grad_all, masked,
     load_sem, send_sem, dec_recv, del_recv, enc_recv, pair_recv, grad_recv, pg_recv, ready_z, ready_xy,
 ):
     levels = n_up // 2
@@ -298,7 +298,7 @@
         masked[...], grad_all[...], (((0,), (0,)), ((), ())), preferred_element_type=F32)
     for s in range(dact):
         prod[s] = whole[:, s * BLOCK:(s + 1) * BLOCK]
-    prod[dact] = jnp.zeros((rows, BLOCK), F32)
+        table[s] = jnp.full(table.shape[1:], downb[s], jnp.int32)
 
     far = last - z
 
@@ -345,19 +345,6 @@
         pair_copy(enc_all.at[1, enc_b(far, 1 - core)], levels + 1).wait_recv()
         mult(far, everything, 1, (1 - core) * (depth - TAIL), TAIL)
 
-    tile = 64
-    places = []
-    for c in range(blocks):
-        hits = hits_of(c, [downb[s] for s in range(dact)])
-        slot = sum(s * hit for s, hit in enumerate(hits))
-        places.append((within(slot, dact), within(slot + dact * (1 - sum(hits)), dact + 1)))
-
-    @pl.loop(0, rows // tile)
-    def _(t):
-        rs = pl.ds(pl.multiple_of(t * tile, tile), tile)
-        for c, (slot, factor) in enumerate(places):
-            out[rs, c * BLOCK:(c + 1) * BLOCK] = acc[slot, rs] * prod[factor, rs]
-
     def sent(ref, kind):
         pltpu.make_async_copy(ref, ref, send_sem.at[kind]).wait()
 
@@ -375,6 +362,26 @@
     sent(enc_all.at[:, pl.ds(0, levels * height)], 2)
     sent(del_all.at[pl.ds(0, n_down - 1)], 3)
     sent(grad_all.at[pl.ds(0, levels * toks)], 5)
+
+
+def place(acc, prod, table, out, held, sem):
+    dact, rows, _ = acc.shape
+    blocks = out.shape[1] // BLOCK
+    tile = 64
+
+    @pl.loop(0, rows // tile)
+    def _(t):
+        rs = pl.ds(pl.multiple_of(t * tile, tile), tile)
+        values = [acc[s, rs] * prod[s, rs] for s in range(dact)]
+        numbers = [jnp.broadcast_to(table[s, 0:1], (tile, BLOCK)) for s in range(dact)]
+        for c in range(blocks):
+            total = jnp.zeros((tile, BLOCK), F32)
+            for value, number in zip(values, numbers):
+                total = jnp.where(number == c, value, total)
+            held[rs, c * BLOCK:(c + 1) * BLOCK] = total
+        pltpu.make_async_copy(held.at[rs], out.at[rs], sem.at[0]).start()
+
+    pltpu.make_async_copy(held, out, sem.at[0]).wait()
 
 
 def ring_local(n_up, n_down, win, deltas, gradients, up_blocks, down_blocks, decoder, encoder):
@@ -389,11 +396,15 @@
     kind = decoder.dtype
     dma = pltpu.SemaphoreType.DMA
     hbm = pl.BlockSpec(memory_space=pltpu.HBM)
-    return pl.pallas_call(
+    vmem = pl.BlockSpec(memory_space=pltpu.VMEM)
+    acc, prod, table = pl.pallas_call(
         functools.partial(gather_scores, n_up, n_down),
-        out_shape=jax.ShapeDtypeStruct((rows, cols), F32),
+        out_shape=[
+            jax.ShapeDtypeStruct((dact, rows, BLOCK), F32), jax.ShapeDtypeStruct((dact, rows, BLOCK), F32),
+            jax.ShapeDtypeStruct((dact, 8, BLOCK), jnp.int32),
+        ],
         in_specs=[hbm] * 6,
-        out_specs=pl.BlockSpec(memory_space=pltpu.VMEM),
+        out_specs=[vmem] * 3,
         scratch_shapes=[
             pltpu.SMEM((uact, up_blocks.shape[0]), jnp.int32),
             pltpu.SMEM((dact,), jnp.int32),
@@ -405,8 +416,6 @@
             pltpu.VMEM((cols // BLOCK, toks, BLOCK), kind),
             pltpu.VMEM((n_up * toks, used), kind),
             pltpu.VMEM((tokens, rows), kind),
-            pltpu.VMEM((dact, rows, BLOCK), F32),
-            pltpu.VMEM((dact + 1, rows, BLOCK), F32),
             dma((6,)),
             dma((6,)),
             dma((4,)),
@@ -421,6 +430,15 @@
         compiler_params=pltpu.CompilerParams(collective_id=0, has_side_effects=True, vmem_limit_bytes=LARGE),
         name="gather_scores",
     )(*[pltpu.with_memory_space_constraint(x, pltpu.HBM) for x in (up_blocks.T, down_blocks, deltas, gradients, decoder, encoder)])
+    return pl.pallas_call(
+        place,
+        out_shape=jax.ShapeDtypeStruct((rows, cols), F32),
+        in_specs=[vmem] * 3,
+        out_specs=hbm,
+        scratch_shapes=[pltpu.VMEM((rows, cols), F32), dma((1,))],
+        compiler_params=pltpu.CompilerParams(vmem_limit_bytes=SMALL),
+        name="place",
+    )(acc, prod, table)
 
 
 def plain_local(deltas, gradients, up_blocks, down_blocks, decoder, encoder):

time: 48.1 us -> 47.8 us (level)
  local copies, waits for them, and re-layouts: 1.32 us -> 0 us
  Pallas kernels: 46.6 us -> 47.6 us
    pallas_call x0 -> x1, Pallas kernels: none -> 1.36 us  [ring_local(): pl.pallas_call(place, out_shape=jax.ShapeDtypeStruct((rows, cols), F32),...]
    unnamed x1 -> x0, local copies, waits for them, and re-layouts: 1.32 us -> none
where the time goes in v9:
time: 47.8 us; the launch traced here: 47.6 us
  Pallas kernels  47.6 us (100%)
    pallas_call x1, Pallas kernels, ring_local(): pl.pallas_call(functools.partial(gather_scores, n_up, n_down), out_shape=...  46.2 us
    pallas_call x1, Pallas kernels, ring_local(): pl.pallas_call(place, out_shape=jax.ShapeDtypeStruct((rows, cols), F32),...  1.36 us

profile of v9, /device:TPU:0, one launch (start us, length us, event | category | flops | bytes accessed | tf_op | source)
XLA Modules:
  0.0 47.6 jit_solution(4355732523034912155)
XLA Ops:
  0.0 46.2 %gather_scores.1 = (f32[4,512,128]{2,1,0:T(8,128)S(1)}, f32[4,512,128]{2,1,0:T(8,128)S(1)}, s32[4,8,128]{2,1,0:T(8,128)S(1)}) custom-call(s32[2,8]{1,0:T(2,128)} %bitcast.1, s32[4]{0:T(128)} %downb_in.1, bf16[64,512]{1,0:T(8,128)(2,1)} %deltas.1, bf16[32,1024]{1,0:T(8,128)(2,1)} %grads.1, bf16[512,1152]{1,0:T(8,128)(2,1)} %dec.1, bf16[576,1024]{1,0:T(8,128)(2,1)} %enc.1), custom_call_target="tpu_custom_call" | custom-call | tf_op jit(solution)/shard_map/gather_scores/pallas_call | solution.py:400
  46.2 1.4 %place.1 = f32[512,1024]{1,0:T(8,128)} custom-call(f32[4,512,128]{2,1,0:T(8,128)S(1)} %get-tuple-element.8.acc, f32[4,512,128]{2,1,0:T(8,128)S(1)} %get-tuple-element.9.prod, s32[4,8,128]{2,1,0:T(8,128)S(1)} %get-tuple-element.10.table), custom_call_target="tpu_custom_call" | custom-call | tf_op jit(solution)/shard_map/place/pallas_call | solution.py:433

commit v10 on v9

--- a/solution.py
+++ b/solution.py
@@ -118,22 +118,22 @@
 
     def del_copy(r, owner):
         ref = del_all.at[owner]
-        return remote(ref, ref, 3, del_recv.at[0], ring_to[r])
+        return remote(ref, ref, 0, del_recv.at[0], ring_to[r])
 
     def del_relay(r, owner):
         ref = del_all.at[owner, r]
-        return remote(ref, ref, 3, del_recv.at[1], ring_to[r])
+        return remote(ref, ref, 0, del_recv.at[1], ring_to[r])
 
     def grad_rows(level, c):
         return grad_all.at[pl.ds(pl.multiple_of((level * 2 + c) * toks, toks), toks)]
 
     def grad_copy(r, level):
         ref = grad_rows(level, core)
-        return remote(ref, ref, 4, grad_recv.at[level], (up + 2 * step_of[r], down))
+        return remote(ref, ref, 1, grad_recv.at[level], (up + 2 * step_of[r], down))
 
     def pair_grad(level):
         ref = grad_rows(level, core)
-        return remote(ref, ref, 5, pg_recv.at[0], pair)
+        return remote(ref, ref, 2, pg_recv.at[0], pair)
 
     def pick_enc(h):
         for s in range(h * dact // 2, (h + 1) * dact // 2):
@@ -348,26 +348,23 @@
     def sent(ref, kind):
         pltpu.make_async_copy(ref, ref, send_sem.at[kind]).wait()
 
-    sent(dec_all.at[pl.ds(0, 3)], 0)
+    both = height + toks
+    sent(enc_all.at[:, pl.ds(0, (n_down - 1) * (rows * depth + wins * uact * win * BLOCK) // (2 * half))], 0)
 
     @pl.when(at_end)
     def _():
-        sent(enc_all.at[:, pl.ds(0, height)], 1)
-        sent(grad_all.at[pl.ds(0, toks)], 4)
+        sent(enc_all.at[:, pl.ds(0, both)], 1)
 
     @pl.when(jnp.logical_not(at_end))
     def _():
-        sent(enc_all.at[:, pl.ds(0, (levels + 1) * height)], 1)
-        sent(grad_all.at[pl.ds(0, (levels + 1) * toks)], 4)
-    sent(enc_all.at[:, pl.ds(0, levels * height)], 2)
-    sent(del_all.at[pl.ds(0, n_down - 1)], 3)
-    sent(grad_all.at[pl.ds(0, levels * toks)], 5)
+        sent(enc_all.at[:, pl.ds(0, (levels + 1) * both)], 1)
+    sent(enc_all.at[:, pl.ds(0, levels * both)], 2)
 
 
 def place(acc, prod, table, out, held, sem):
     dact, rows, _ = acc.shape
     blocks = out.shape[1] // BLOCK
-    tile = 64
+    tile = 32
 
     @pl.loop(0, rows // tile)
     def _(t):
@@ -417,7 +414,7 @@
             pltpu.VMEM((n_up * toks, used), kind),
             pltpu.VMEM((tokens, rows), kind),
             dma((6,)),
-            dma((6,)),
+            dma((3,)),
             dma((4,)),
             dma((2,)),
             dma((2 * levels + 1,)),

time: 47.8 us -> 47.7 us (level)
  no operation moved by 1% of the time
where the time goes in v10:
time: 47.7 us; the launch traced here: 47.5 us
  Pallas kernels  47.5 us (100%)
    pallas_call x1, Pallas kernels, ring_local(): pl.pallas_call(functools.partial(gather_scores, n_up, n_down), out_shape=...  46.2 us
    pallas_call x1, Pallas kernels, ring_local(): pl.pallas_call(place, out_shape=jax.ShapeDtypeStruct((rows, cols), F32),...  1.33 us

profile of v10, /device:TPU:0, one launch (start us, length us, event | category | flops | bytes accessed | tf_op | source)
XLA Modules:
  0.0 47.5 jit_solution(2229253995358743058)
XLA Ops:
  0.0 46.2 %gather_scores.1 = (f32[4,512,128]{2,1,0:T(8,128)S(1)}, f32[4,512,128]{2,1,0:T(8,128)S(1)}, s32[4,8,128]{2,1,0:T(8,128)S(1)}) custom-call(s32[2,8]{1,0:T(2,128)} %bitcast.1, s32[4]{0:T(128)} %downb_in.1, bf16[64,512]{1,0:T(8,128)(2,1)} %deltas.1, bf16[32,1024]{1,0:T(8,128)(2,1)} %grads.1, bf16[512,1152]{1,0:T(8,128)(2,1)} %dec.1, bf16[576,1024]{1,0:T(8,128)(2,1)} %enc.1), custom_call_target="tpu_custom_call" | custom-call | tf_op jit(solution)/shard_map/gather_scores/pallas_call | solution.py:397
  46.2 1.3 %place.1 = f32[512,1024]{1,0:T(8,128)} custom-call(f32[4,512,128]{2,1,0:T(8,128)S(1)} %get-tuple-element.8.acc, f32[4,512,128]{2,1,0:T(8,128)S(1)} %get-tuple-element.9.prod, s32[4,8,128]{2,1,0:T(8,128)S(1)} %get-tuple-element.10.table), custom_call_target="tpu_custom_call" | custom-call | tf_op jit(solution)/shard_map/place/pallas_call | solution.py:430

commit v11 on v10

--- a/solution.py
+++ b/solution.py
@@ -366,9 +366,8 @@
     blocks = out.shape[1] // BLOCK
     tile = 32
 
-    @pl.loop(0, rows // tile)
-    def _(t):
-        rs = pl.ds(pl.multiple_of(t * tile, tile), tile)
+    for t in range(rows // tile):
+        rs = slice(t * tile, (t + 1) * tile)
         values = [acc[s, rs] * prod[s, rs] for s in range(dact)]
         numbers = [jnp.broadcast_to(table[s, 0:1], (tile, BLOCK)) for s in range(dact)]
         for c in range(blocks):

time: 47.7 us -> 47.7 us (level)
  no operation moved by 1% of the time
where the time goes in v11:
time: 47.7 us; the launch traced here: 47.5 us
  Pallas kernels  47.5 us (100%)
    pallas_call x1, Pallas kernels, ring_local(): pl.pallas_call(functools.partial(gather_scores, n_up, n_down), out_shape=...  46.2 us
    pallas_call x1, Pallas kernels, ring_local(): pl.pallas_call(place, out_shape=jax.ShapeDtypeStruct((rows, cols), F32),...  1.33 us

profile of v11, /device:TPU:0, one launch (start us, length us, event | category | flops | bytes accessed | tf_op | source)
XLA Modules:
  0.0 47.5 jit_solution(16797454346066570490)
XLA Ops:
  0.0 46.2 %gather_scores.1 = (f32[4,512,128]{2,1,0:T(8,128)S(1)}, f32[4,512,128]{2,1,0:T(8,128)S(1)}, s32[4,8,128]{2,1,0:T(8,128)S(1)}) custom-call(s32[2,8]{1,0:T(2,128)} %bitcast.1, s32[4]{0:T(128)} %downb_in.1, bf16[64,512]{1,0:T(8,128)(2,1)} %deltas.1, bf16[32,1024]{1,0:T(8,128)(2,1)} %grads.1, bf16[512,1152]{1,0:T(8,128)(2,1)} %dec.1, bf16[576,1024]{1,0:T(8,128)(2,1)} %enc.1), custom_call_target="tpu_custom_call" | custom-call | tf_op jit(solution)/shard_map/gather_scores/pallas_call | solution.py:396
  46.2 1.3 %place.1 = f32[512,1024]{1,0:T(8,128)} custom-call(f32[4,512,128]{2,1,0:T(8,128)S(1)} %get-tuple-element.8.acc, f32[4,512,128]{2,1,0:T(8,128)S(1)} %get-tuple-element.9.prod, s32[4,8,128]{2,1,0:T(8,128)S(1)} %get-tuple-element.10.table), custom_call_target="tpu_custom_call" | custom-call | tf_op jit(solution)/shard_map/place/pallas_call | solution.py:429
